TPU v7x, 128 devices: a whole 4x4x4 slice. The times are simulated.
128 devices in a mesh: rows: 32 (over y_hi, z, x), tm: 4 (over y_lo, core).
Axes of the slice: x: 4, y: 4 (y_hi: 2, y_lo: 2; y = y_hi * 2 + y_lo), z: 4, core: 2. Of those that a mesh axis runs over, the one named last changes fastest.
Arguments:
- snapshots: bfloat16 [1048576, 512], P('rows', 'tm'), may hold values from -6 to 6
- modes: bfloat16 [1048576, 256], P('rows'), may hold values from -0.005859375 to 0.005859375
- eig_vectors: float32 [3, 256], replicated, may hold values from -0.375 to 0.375
- eig_values: float32 [3], replicated, may hold values from -1 to 1
Outputs:
- operator: float32 [256, 256], replicated
- eig_residual: float32 [3, 256], replicated
- residual_norm: float32 [3], replicated
All inputs are finite; a program needn't handle non-finite values.
Results may differ from a plain program's by a relative error of at most 0.0003.
Values may be sent and summed in bfloat16 or wider, within the bound.
No kernel may reach another device: no remote copies, remote signals or barrier semaphores. Data moves between devices by JAX's collectives and lax.ppermute only.
A program may use at most 128 MiB of HBM per device.

v0:
```python
import jax
import jax.numpy as jnp
from jax import lax
from jax.sharding import PartitionSpec as P


def cut_along(array, dim, devices):
    before, after = (array.shape[:dim], array.shape[dim + 1 :])
    return jnp.moveaxis(array.reshape(*before, devices, -1, *after), dim, 0)


def summed_on_arrival(array, axis, dim):
    devices = lax.axis_size(axis)
    blocks = lax.all_to_all(cut_along(array, dim, devices), axis, 0, 0, tiled=True)
    return jnp.sum(blocks, axis=0)


def rows_for(lines, devices):
    spare = -lines.shape[0] % devices
    if not spare:
        return lines
    return jnp.concatenate([lines, jnp.zeros((spare, *lines.shape[1:]), lines.dtype)])


def in_order(blocks, dim):
    blocks = jnp.moveaxis(blocks, 0, dim)
    dims = blocks.shape
    return blocks.reshape(*dims[:dim], dims[dim] * dims[dim + 1], *dims[dim + 2 :])


def from_everyone(array, axis):
    devices = lax.axis_size(axis)
    return lax.all_to_all(
        jnp.broadcast_to(array[None], (devices, *array.shape)), axis, 0, 0, tiled=True
    )


def gathered_copies(array, axis, dim):
    return in_order(from_everyone(array, axis), dim)


def nested_sum(array, axes):
    lines = array.reshape(-1, array.shape[-1])
    own = summed_on_arrival(rows_for(lines, lax.axis_size(axes)), axes, 0)
    whole = gathered_copies(own, axes, 0)
    return whole[: len(lines)].reshape(array.shape)


def pair_terms(coords, after, keep):
    lead = coords * keep
    trail = jnp.concatenate([coords[:, 1:], after], axis=1)
    cross_part = jnp.dot(
        trail, lead.T, precision=lax.Precision.HIGHEST, preferred_element_type=jnp.float32
    )
    gram_part = jnp.dot(
        lead, lead.T, precision=lax.Precision.HIGHEST, preferred_element_type=jnp.float32
    )
    return (cross_part, gram_part)


def body(snapshots, modes, eig_vectors, eig_values):
    block_cols = snapshots.shape[1]
    width = modes.shape[1]
    time_count = lax.axis_size("tm")
    total_cols = block_cols * time_count
    partial_value = jnp.einsum("mr,mt->rt", modes, snapshots, preferred_element_type=jnp.float32)
    coords = nested_sum(partial_value, "rows")
    series = gathered_copies(coords, "tm", 1)
    every = lax.broadcasted_iota(jnp.int32, (1, total_cols), 1)
    whole_keep = (every < total_cols - 1).astype(jnp.float32)
    zero_col = jnp.zeros((width, 1), jnp.float32)
    cross, gram = pair_terms(series, zero_col, whole_keep)
    scale = jnp.float32(total_cols - 1)
    cross = cross / scale
    gram = gram / scale + jnp.eye(width, dtype=jnp.float32)
    factor = jnp.linalg.cholesky(gram)
    operator = jax.scipy.linalg.cho_solve((factor, True), cross.T).T
    eig_residual = (
        jnp.dot(
            eig_vectors,
            operator.T,
            precision=lax.Precision.HIGHEST,
            preferred_element_type=jnp.float32,
        )
        - eig_values[:, None] * eig_vectors
    )
    residual_norm = jnp.sqrt(jnp.sum(eig_residual * eig_residual, axis=1) + 1e-06)
    return (operator, eig_residual, residual_norm)


def solution(mesh):
    return jax.shard_map(
        body,
        mesh=mesh,
        in_specs=(P("rows", "tm"), P("rows", None), P(), P()),
        out_specs=(P(), P(), P()),
        check_vma=False,
    )
```

profile of v0, /device:TPU:1, one launch (start us, length us, event | category | flops | bytes accessed | tf_op | source)
XLA Modules:
  0.0 125.8 jit_solution(16588956966764815971)
XLA Ops:
  0.7 10.6 %convolution_bitcast_fusion.1 = f32[32,8,128]{2,1,0:T(8,128)S(1)} fusion(bf16[32768,256]{1,0:T(8,128)(2,1)} %param.5, bf16[32768,128]{1,0:T(8,128)(2,1)} %param.4), kind=kOutput, calls=%fused_computation.7 | convolution fusion | flops 2147483648 | bytes 25296896 | tf_op jit(solution)/shard_map/mr,mt->rt/dot_general | solution.py:66
  11.3 19.9 %all_to_all.15 = f32[32,8,128]{2,1,0:T(8,128)S(1)} all-to-all(f32[32,8,128]{2,1,0:T(8,128)S(1)} %convolution_bitcast_fusion.1), channel_id=1, replica_groups=mesh['rows'=32,'tm'=4] {'rows'}, dimensions={0} | all-to-all | bytes 262144 | tf_op jit(solution)/shard_map/all_to_all | solution.py:14
  31.3 12.4 %all_to_all.16 = f32[32,8,128]{2,1,0:T(8,128)S(1)} all-to-all(f32[32,8,128]{2,1,0:T(8,128)S(1)} %broadcast_in_dim.7), channel_id=1, replica_groups=mesh['rows'=32,'tm'=4] {'rows'}, dimensions={0} | all-to-all | bytes 262144 | tf_op jit(solution)/shard_map/all_to_all | solution.py:33
  43.6 0.1 copy.17
  43.7 0.8 broadcast_in_dim.10
  44.5 6.8 %all-to-all-start.2 = ((f32[4,256,128]{1,2,0:T(8,128)}), f32[4,256,128]{1,2,0:T(8,128)S(1)}, u32[]{:S(2)}, u32[]{:S(2)}) async-start(f32[4,256,128]{1,2,0:T(8,128)} %broadcast_in_dim.10), calls=%async_computation.2 | async-start | bytes 1048576 | tf_op jit(solution)/shard_map/all_to_all | solution.py:33
  51.4 7.8 %all-to-all-done.2 = f32[4,256,128]{1,2,0:T(8,128)S(1)} async-done(((f32[4,256,128]{1,2,0:T(8,128)}), f32[4,256,128]{1,2,0:T(8,128)S(1)}, u32[]{:S(2)}, u32[]{:S(2)}) %all-to-all-start.2) | async-done | bytes 524320 | tf_op jit(solution)/shard_map/all_to_all | solution.py:33
  59.2 1.2 convert_add_fusion
  60.4 0.1 copy.21
  60.6 11.7 %cholesky.50 = f32[128,128]{1,0:T(8,128)S(1)} custom-call(f32[128,128]{1,0:T(8,128)S(1)} %cholesky.118), custom_call_target="Cholesky" | custom-call | tf_op jit(solution)/shard_map/jit(cholesky)/cholesky | solution.py:76
  72.4 9.8 %custom-call.18 = f32[1,128,128]{1,2,0:T(8,128)S(1)} custom-call(f32[1,128,128]{2,1,0:T(8,128)S(1)} %get-tuple-element.33), custom_call_target="InvertDiagBlocksLowerTriangular" | custom-call | tf_op jit(solution)/shard_map/jit(cholesky)/cholesky | solution.py:76
  82.2 0.2 constant_dynamic-update-slice_fusion.1
  82.4 0.3 convolution_subtract_fusion.2
  82.7 11.7 %cholesky.105 = f32[128,128]{1,0:T(8,128)S(1)} custom-call(f32[128,128]{1,0:T(8,128)S(1)} %convolution_subtract_fusion.2), custom_call_target="Cholesky" | custom-call | tf_op jit(solution)/shard_map/jit(cholesky)/cholesky | solution.py:76
  94.5 0.6 compare_reduce_fusion
  96.4 0.1 triangular_solve.72
  96.5 4.0 %while.1 = (s32[]{:T(128)}, f32[256,256]{1,0:T(8,128)S(1)}, s32[2,2]{1,0:T(2,128)S(1)}, f32[2,128,128]{2,1,0:T(8,128)S(1)}, s32[]{:T(128)}) while((s32[]{:T(128)}, f32[256,256]{1,0:T(8,128)S(1)}, s32[2,2]{1,0:T(2,128)S(1)}, f32[2,128,128]{2,1,0:T(8,128)S(1)}, s32[]{:T(128)}) %tuple.32), condition=%wide.while_cond, body=%wide.while_body.sunk | while | flops 2 | bytes 131189 | solution.py:77
  96.5 0.6 fusion.35
  97.1 1.4 %bitcast_dynamic-update-slice_fusion.2 = f32[2,128,128]{2,1,0:T(8,128)S(1)} fusion(f32[2,128,128]{2,1,0:T(8,128)S(1)} %get-tuple-element.79, s32[]{:T(128)S(6)} %copy.36, f32[256,256]{1,0:T(8,128)S(1)} %get-tuple-element.82, s32[]{:T(128)} %bitcast.59, s32[]{:T(128)} %bitcast.60), kind=kLoop, calls=%fused_computation.clone.1 | loop fusion | bytes 131084 | tf_op jit(solution)/shard_map/jit(_cho_solve)/triangular_solve
  98.5 0.6 fusion.35
  99.1 1.4 %bitcast_dynamic-update-slice_fusion.2 = f32[2,128,128]{2,1,0:T(8,128)S(1)} fusion(f32[2,128,128]{2,1,0:T(8,128)S(1)} %get-tuple-element.79, s32[]{:T(128)S(6)} %copy.36, f32[256,256]{1,0:T(8,128)S(1)} %get-tuple-element.82, s32[]{:T(128)} %bitcast.59, s32[]{:T(128)} %bitcast.60), kind=kLoop, calls=%fused_computation.clone.1 | loop fusion | bytes 131084 | tf_op jit(solution)/shard_map/jit(_cho_solve)/triangular_solve
  100.5 19.9 %custom-call.19 = f32[2,128,128]{1,2,0:T(8,128)S(1)} custom-call(f32[2,128,128]{2,1,0:T(8,128)S(1)} %get-tuple-element.10), custom_call_target="InvertDiagBlocksLowerTriangular" | custom-call | tf_op jit(solution)/shard_map/jit(_cho_solve)/triangular_solve | solution.py:77
  120.4 1.1 convolution_multiply_fusion
  121.5 0.3 fusion.9
  121.8 0.4 convolution_subtract_fusion.1
  122.2 0.3 fusion.16
  122.5 0.3 fusion.15
  122.8 0.3 convolution_subtract_fusion
  123.1 0.3 fusion.14
  123.4 0.8 copy.24
  124.3 1.0 multiply_reduce_fusion
  125.2 0.5 add_sqrt_fusion
  (20 shorter events, 0.3 us)
Async XLA Ops:
  0.6 123.6 %copy-start = (f32[3,256]{1,0:T(4,128)S(1)}, f32[3,256]{1,0:T(4,128)}, u32[]{:S(2)}) copy-start(f32[3,256]{1,0:T(4,128)} %param.6) | copy-start | bytes 9220
  0.6 123.6 %copy-start.1 = (f32[3]{0:T(128)S(1)}, f32[3]{0:T(128)}, u32[]{:S(2)}) copy-start(f32[3]{0:T(128)} %param.7) | copy-start | bytes 40
  44.5 14.7 %all-to-all-start.2 = ((f32[4,256,128]{1,2,0:T(8,128)}), f32[4,256,128]{1,2,0:T(8,128)S(1)}, u32[]{:S(2)}, u32[]{:S(2)}) async-start(f32[4,256,128]{1,2,0:T(8,128)} %broadcast_in_dim.10), calls=%async_computation.2 | async-start | bytes 1048576 | tf_op jit(solution)/shard_map/all_to_all | solution.py:33
where the time goes:
time: 126 us
  other arithmetic  54.5 us (43%)
  blocking collectives  32.3 us (26%)
  matrix products  16.1 us (13%)
  waiting for transfers between devices  7.83 us (6%)
  starting transfers between devices  6.84 us (5%)
  local copies, waits for them, and re-layouts  6 us (5%)
  between operations  2.12 us (2%)
    another operation x6, other arithmetic, body(): factor = jnp.linalg.cholesky(gram)  33.9 us
    all_to_all x1, blocking collectives, summed_on_arrival(): lax.all_to_all(cut_along(array, dim, devices), axis, 0, 0, tiled=True)  19.9 us
    another operation x3, other arithmetic, body(): operator = jax.scipy.linalg.cho_solve((factor, True), cross.T).T  19.9 us
    all_to_all x1, blocking collectives, from_everyone(): lax.all_to_all(jnp.broadcast_to(array[None], (devices, *array.shape)), ax...  12.4 us
    dot_general x1, matrix products, body(): jnp.einsum('mr,mt->rt', modes, snapshots, preferred_element_type=jnp.floa...  10.6 us
    all_to_all x1, waiting for transfers between devices, from_everyone(): lax.all_to_all(jnp.broadcast_to(array[None], (devices, *array.shape)), ax...  7.83 us
    all_to_all x1, starting transfers between devices, from_everyone(): lax.all_to_all(jnp.broadcast_to(array[None], (devices, *array.shape)), ax...  6.84 us
    another operation x6, local copies, waits for them, and re-layouts  3.95 us
  transfers between devices with their start and end apart: 1, of which 1 were waited for; matrix products, arithmetic and copies ran while one was open for 0% of the time, Pallas kernels for 0%

commit v1 on v0

v1 whole, which is shorter than its diff:
```python
import functools

import jax
import jax.numpy as jnp
from jax import lax
from jax.experimental import pallas as pl
from jax.experimental.pallas import tpu as pltpu
from jax.sharding import PartitionSpec as P

LARGEST_FAST = 2048.0
RESIDUAL_FLOOR = 224.0


def pieces(array):
    high = array.astype(jnp.bfloat16)
    low = (array - high.astype(jnp.float32)).astype(jnp.bfloat16)
    return high, low


def dot3(left, right):
    left_high, left_low = left
    right_high, right_low = right
    mm = functools.partial(jnp.dot, preferred_element_type=jnp.float32)
    return mm(left_high, right_high) + (mm(left_high, right_low) + mm(left_low, right_high))


def dot_full(left, right, contract=((1,), (0,))):
    return lax.dot_general(
        left,
        right,
        (contract, ((), ())),
        precision=lax.Precision.HIGHEST,
        preferred_element_type=jnp.float32,
    )


def eliminate(gram_ref, work, width):
    lanes = lax.broadcasted_iota(jnp.int32, (1, 2 * width), 1)
    lines = lax.broadcasted_iota(jnp.int32, (width, 1), 0)

    def step(k, carry):
        row = work[pl.ds(k, 1), :]
        here = (lanes == k).astype(jnp.float32)
        pivot = jnp.sum(row * here, axis=1, keepdims=True)
        row = row / pivot
        column = jnp.sum(work[...] * here, axis=1, keepdims=True)
        on_line = lines == k
        work[...] = jnp.where(on_line, row, work[...] - column * row)
        return carry

    lax.fori_loop(0, width, step, 0)


def solve_kernel(core_ref, own_ref, other_ref, vec_ref, val_ref, op_out, res_ref, norm_ref,
                 gram_ref, cross_ref, r_ref, x_ref, op_ref, work, sem):
    width = gram_ref.shape[0]
    first = core_ref[0] == 0
    blocks = []
    for half in range(2):
        own = own_ref[:, half].reshape(width, 128)
        other = other_ref[:, half].reshape(width, 128)
        blocks.append(jnp.where(first, own, other))
        blocks.append(jnp.where(first, other, own))
    series = jnp.concatenate(blocks, axis=1)
    total = series.shape[1]
    scale = 1.0 / (total - 1)
    column = lax.broadcasted_iota(jnp.int32, (1, total), 1)
    lead = jnp.where(column < total - 1, series, 0.0)
    trail = pltpu.roll(series, total - 1, 1)
    both = dot_full(jnp.concatenate([lead, trail], axis=0), lead, ((1,), (1,)))
    eye = (
        lax.broadcasted_iota(jnp.int32, (width, width), 0)
        == lax.broadcasted_iota(jnp.int32, (width, width), 1)
    ).astype(jnp.float32)
    gram = both[:width] * scale + eye
    cross = both[width:] * scale
    gram_ref[...] = gram
    cross_ref[...] = cross

    gram_pieces = pieces(gram)
    square = dot3(gram_pieces, gram_pieces)
    top = jnp.max(jnp.sum(jnp.abs(square), axis=0, keepdims=True))
    top = jnp.maximum(jnp.sqrt(jnp.full((8, 128), top, jnp.float32)) * 1.001, 1.5)
    bound = jnp.max(top)

    @pl.when(bound <= LARGEST_FAST)
    def _():
        alpha = 2.0 / (top + 1.0)
        t1 = (top + 1.0) / (top - 1.0)
        t2 = 2.0 * t1 * t1 - 1.0
        inv2 = 1.0 / t2
        a = alpha[:1, :1]
        i2 = inv2[:1, :1]
        c = 1.0 + i2
        r_ref[...] = c * (eye - (2.0 * a) * gram_ref[...] + (a * a) * square) - i2 * eye
        x_ref[...] = (c * a) * (2.0 * eye - a * gram_ref[...])

        def more(state):
            return jnp.max(2.0 * state * state - 1.0) < RESIDUAL_FLOOR

        def double(t):
            t = 2.0 * t * t - 1.0
            it = (1.0 / t)[:1, :1]
            r = r_ref[...]
            x = x_ref[...]
            rp = pieces(r)
            x_ref[...] = (1.0 + it) * (x + dot3(pieces(x), rp))
            r_ref[...] = (1.0 + it) * dot3(rp, rp) - it * eye
            return t

        t = lax.while_loop(more, double, t2)
        t = 2.0 * t * t - 1.0
        it = (1.0 / t)[:1, :1]
        x = x_ref[...]
        x = (1.0 + it) * (x + dot3(pieces(x), pieces(r_ref[...])))
        xp = pieces(x)
        x_ref[...] = x

        def refine(guess):
            rest = cross_ref[...] - dot_full(guess, gram_ref[...])
            return guess + dot3(pieces(rest), xp)

        last = 1.0 + (1.0 / (2.0 * t * t - 1.0))[:1, :1]
        guess = dot3(pieces(cross_ref[...]), xp)
        op_ref[...] = last * refine(guess)

        @pl.when(bound > 32.0)
        def _():
            for _ in range(3):
                op_ref[...] = refine(op_ref[...])

    @pl.when(bound > LARGEST_FAST)
    def _():
        work[:, :width] = gram_ref[...]
        work[:, width:] = cross_ref[...].T
        eliminate(gram_ref, work, width)
        op_ref[...] = work[:, width:].T

    out = pltpu.make_async_copy(op_ref, op_out, sem)
    out.start()
    vectors = vec_ref[...]
    residual = dot_full(vectors, op_ref[...], ((1,), (1,))) - val_ref[...] * vectors
    res_ref[...] = residual
    norm_ref[...] = jnp.sqrt(jnp.sum(residual * residual, axis=1, keepdims=True) + 1e-06)
    out.wait()


def solve(core, own, other, vectors, values):
    eigs, width = vectors.shape
    vmem = pl.BlockSpec(memory_space=pltpu.VMEM)
    square = pltpu.VMEM((width, width), jnp.float32)
    operator, residual, norm = pl.pallas_call(
        solve_kernel,
        out_shape=(
            jax.ShapeDtypeStruct((width, width), jnp.float32),
            jax.ShapeDtypeStruct((eigs, width), jnp.float32),
            jax.ShapeDtypeStruct((eigs, 1), jnp.float32),
        ),
        in_specs=[pl.BlockSpec(memory_space=pltpu.SMEM), vmem, vmem, vmem, vmem],
        out_specs=(pl.BlockSpec(memory_space=pl.ANY), vmem, vmem),
        scratch_shapes=[square] * 5
        + [pltpu.VMEM((width, 2 * width), jnp.float32), pltpu.SemaphoreType.DMA],
        name="solve",
    )(core, own, other, vectors, values[:, None])
    return operator, residual, norm[:, 0]


def joint_groups():
    rows, halves = 32, 2
    return [[r * 4 + 2 * half + core for r in range(rows) for half in range(halves)] for core in range(2)]


def body(snapshots, modes, eig_vectors, eig_values):
    width = modes.shape[1]
    block_cols = snapshots.shape[1]
    rows = lax.axis_size("rows")
    partial_value = jnp.einsum("mr,mt->rt", modes, snapshots, preferred_element_type=jnp.float32)
    lines = width // rows
    arrived = lax.all_to_all(
        partial_value.reshape(rows, lines, block_cols), "rows", 0, 0, tiled=True
    )
    own_lines = jnp.sum(arrived, axis=0)
    axes = ("rows", "tm")
    gathered = lax.all_to_all(
        jnp.broadcast_to(own_lines[None], (2 * rows, lines, block_cols)),
        axes,
        0,
        0,
        tiled=True,
        axis_index_groups=joint_groups(),
    )
    swap = [(i, i ^ 1) for i in range(4 * rows)]
    other = lax.ppermute(gathered, axes, swap)
    core = (lax.axis_index("tm") % 2).astype(jnp.int32).reshape(1)
    shape = (rows, 2, lines, block_cols)
    return solve(core, gathered.reshape(shape), other.reshape(shape), eig_vectors, eig_values)


def solution(mesh):
    return jax.shard_map(
        body,
        mesh=mesh,
        in_specs=(P("rows", "tm"), P("rows", None), P(), P()),
        out_specs=(P(), P(), P()),
        check_vma=False,
    )
```

time: 126 us -> 59.1 us (0.47); the launches traced: 126 us -> 60.1 us
  other arithmetic: 54.5 us -> 1.34 us
  Pallas kernels: 0 us -> 8.77 us
  waiting for transfers between devices: 7.83 us -> 0.48 us
  matrix products: 16.1 us -> 10.6 us
  local copies, waits for them, and re-layouts: 6 us -> 1.4 us
  starting transfers between devices: 6.84 us -> 3.44 us
  between operations: 2.12 us -> 0.66 us
    another operation x9 -> x0, other arithmetic: 53.9 us -> none  [the longest x6 33.9 us: body(): factor = jnp.linalg.cholesky(gram)]
    pallas_call x0 -> x1, Pallas kernels: none -> 8.77 us  [solve(): pl.pallas_call(solve_kernel, out_shape=(jax.ShapeDtypeStruct((width, widt...]
    all_to_all x1 -> x0, waiting for transfers between devices: 7.83 us -> none  [from_everyone(): lax.all_to_all(jnp.broadcast_to(array[None], (devices, *array.shape)), ax...]
    all_to_all x1 -> x0, starting transfers between devices: 6.84 us -> none  [from_everyone(): lax.all_to_all(jnp.broadcast_to(array[None], (devices, *array.shape)), ax...]
    another operation x9 -> x0, local copies, waits for them, and re-layouts: 4.05 us -> none
    ppermute x0 -> x1, starting transfers between devices: none -> 3.44 us  [body(): other = lax.ppermute(gathered, axes, swap)]
    dot_general x3 -> x0, matrix products: 3.21 us -> none  [the longest x1 1.16 us: pair_terms(): jnp.dot(lead, lead.T, precision=lax.Precision.HIGHEST, preferred_element_...]
    another operation x8 -> x0, matrix products: 2.31 us -> none  [the longest x6 1.84 us: body(): operator = jax.scipy.linalg.cho_solve((factor, True), cross.T).T]
  transfers between devices with their start and end apart: 1 -> 1, of which waited for: 1 -> 1; matrix products, arithmetic and copies ran while one was open for 0% -> 1% of each run, Pallas kernels for 0% -> 0%
where the time goes in v1:
time: 59.1 us; the launch traced here: 60.1 us
  blocking collectives  33.4 us (57%)
  matrix products  10.6 us (18%)
  Pallas kernels  8.77 us (15%)
  starting transfers between devices  3.44 us (6%)
  local copies, waits for them, and re-layouts  1.4 us (2%)
  other arithmetic  1.34 us (2%)
  between operations  0.66 us (1%)
    all_to_all x1, blocking collectives, body(): lax.all_to_all(partial_value.reshape(rows, lines, block_cols), 'rows', 0,...  19.9 us
    all_to_all x1, blocking collectives, body(): lax.all_to_all(jnp.broadcast_to(own_lines[None], (2 * rows, lines, block_...  13.5 us
    dot_general x1, matrix products, body(): jnp.einsum('mr,mt->rt', modes, snapshots, preferred_element_type=jnp.floa...  10.6 us
    pallas_call x1, Pallas kernels, solve(): pl.pallas_call(solve_kernel, out_shape=(jax.ShapeDtypeStruct((width, widt...  8.77 us
    ppermute x1, starting transfers between devices, body(): other = lax.ppermute(gathered, axes, swap)  3.44 us
    pallas_call x1, other arithmetic, solve(): pl.pallas_call(solve_kernel, out_shape=(jax.ShapeDtypeStruct((width, widt...  1.3 us
  transfers between devices with their start and end apart: 1, of which 1 were waited for; matrix products, arithmetic and copies ran while one was open for 1% of the time, Pallas kernels for 0%

profile of v1, /device:TPU:1, one launch (start us, length us, event | category | flops | bytes accessed | tf_op | source)
XLA Modules:
  0.0 60.1 jit_solution(5180342117298209713)
XLA Ops:
  0.6 0.0 copy-start.2
  0.6 10.6 %convolution_bitcast_fusion = f32[32,8,128]{2,1,0:T(8,128)S(1)} fusion(bf16[32768,256]{1,0:T(8,128)(2,1)} %param.5, bf16[32768,128]{1,0:T(8,128)(2,1)} %param.4), kind=kOutput, calls=%fused_computation | convolution fusion | flops 2147483648 | bytes 25296896 | tf_op jit(solution)/shard_map/mr,mt->rt/dot_general | solution.py:177
  11.2 19.9 %all_to_all.10 = f32[32,8,128]{2,1,0:T(8,128)S(1)} all-to-all(f32[32,8,128]{2,1,0:T(8,128)S(1)} %convolution_bitcast_fusion), channel_id=1, replica_groups=mesh['rows'=32,'tm'=4] {'rows'}, dimensions={0} | all-to-all | bytes 262144 | tf_op jit(solution)/shard_map/all_to_all | solution.py:179
  31.3 13.5 %all_to_all.11 = f32[64,8,128]{2,1,0:T(8,128)S(1)} all-to-all(f32[64,8,128]{2,1,0:T(8,128)S(1)} %broadcast_in_dim.4), channel_id=1, replica_groups={{0,2,4,6,8,10,12,14,16,18,20,22,24,26,28,30,32,34,36,38,40,42,44,46,48,..., dimensions={0} | all-to-all | bytes 524288 | tf_op jit(solution)/shard_map/all_to_all | solution.py:184
  44.7 0.0 copy-start
  44.8 3.4 %collective-permute-start = (f32[64,8,128]{2,1,0:T(8,128)S(1)}, f32[64,8,128]{2,1,0:T(8,128)S(1)}, u32[]{:S(2)}, u32[]{:S(2)}) collective-permute-start(f32[64,8,128]{2,1,0:T(8,128)S(1)} %all_to_all.11), channel_id=1, source_target_pairs={{0,1},{1,0},{2,3},{3,2},{4,5},{5,4},{6,7},{7,6},{8,9},{9,8},{10,11... | collective-permute-start | bytes 786440 | tf_op jit(solution)/shard_map/ppermute | solution.py:193
  48.2 0.0 copy-done.2
  48.2 0.7 %copy.8.val_ref = f32[3,1]{1,0:T(4,128)} copy(f32[3,1]{0,1:T(1,128)S(1)} %bitcast.10) | data formatting | bytes 24 | tf_op jit(solution)/shard_map/broadcast_in_dim | solution.py:164
  48.9 0.5 collective-permute-done
  49.4 0.0 copy-start.1
  49.4 0.0 copy-done
  49.4 0.7 %copy-done.1 = f32[64,8,128]{2,1,0:T(8,128)} copy-done((f32[64,8,128]{2,1,0:T(8,128)}, f32[64,8,128]{2,1,0:T(8,128)S(1)}, u32[]{:S(2)}) %copy-start.1) | copy-done | bytes 262168
  50.1 8.8 %solve.1 = (f32[256,256]{1,0:T(8,128)}, f32[3,256]{1,0:T(4,128)}, f32[3,1]{1,0:T(4,128)}) custom-call(s32[1]{0:T(128)} %bitcast.core_ref, f32[32,2,8,128]{3,2,1,0:T(8,128)} %bitcast.8, f32[32,2,8,128]{3,2,1,0:T(8,128)} %bitcast.9, f32[3,256]{1,0:T(4,128)} %vec_ref.1, f32[3,1]{1,0:T(4,128)} %copy.8.val_ref), custom_call_target="tpu_custom_call" | custom-call | tf_op jit(solution)/shard_map/solve/pallas_call | solution.py:152
  58.8 1.3 %reduce = f32[3]{0:T(128)} reduce(f32[3,1]{1,0:T(4,128)} %get-tuple-element.8, f32[]{:T(128)} %constant.19), dimensions={1}, to_apply=%get-tuple-element.8.reduce_sub_computation | reduce | bytes 28 | tf_op jit(solution)/shard_map/solve/pallas_call | solution.py:152
  (2 shorter events, 0.1 us)
Async XLA Ops:
  0.6 47.6 %copy-start.2 = (f32[3]{0:T(128)S(1)}, f32[3]{0:T(128)}, u32[]{:S(2)}) copy-start(f32[3]{0:T(128)} %param.7) | copy-start | bytes 40
  44.7 4.6 %copy-start = (f32[64,8,128]{2,1,0:T(8,128)}, f32[64,8,128]{2,1,0:T(8,128)S(1)}, u32[]{:S(2)}) copy-start(f32[64,8,128]{2,1,0:T(8,128)S(1)} %all_to_all.11) | copy-start | bytes 786436
  44.8 4.6 %collective-permute-start = (f32[64,8,128]{2,1,0:T(8,128)S(1)}, f32[64,8,128]{2,1,0:T(8,128)S(1)}, u32[]{:S(2)}, u32[]{:S(2)}) collective-permute-start(f32[64,8,128]{2,1,0:T(8,128)S(1)} %all_to_all.11), channel_id=1, source_target_pairs={{0,1},{1,0},{2,3},{3,2},{4,5},{5,4},{6,7},{7,6},{8,9},{9,8},{10,11... | collective-permute-start | bytes 786440 | tf_op jit(solution)/shard_map/ppermute | solution.py:193
  49.4 0.7 %copy-start.1 = (f32[64,8,128]{2,1,0:T(8,128)}, f32[64,8,128]{2,1,0:T(8,128)S(1)}, u32[]{:S(2)}) copy-start(f32[64,8,128]{2,1,0:T(8,128)S(1)} %collective-permute-done) | copy-start | bytes 786436

commit v2 on v1

--- a/solution.py
+++ b/solution.py
@@ -51,10 +51,10 @@
     lax.fori_loop(0, width, step, 0)
 
 
-def solve_kernel(core_ref, own_ref, other_ref, vec_ref, val_ref, op_out, res_ref, norm_ref,
+def solve_kernel(core_of, own_ref, other_ref, vec_ref, val_ref, op_out, res_ref, norm_ref,
                  gram_ref, cross_ref, r_ref, x_ref, op_ref, work, sem):
     width = gram_ref.shape[0]
-    first = core_ref[0] == 0
+    first = core_of() == 0
     blocks = []
     for half in range(2):
         own = own_ref[:, half].reshape(width, 128)
@@ -139,30 +139,93 @@
     out = pltpu.make_async_copy(op_ref, op_out, sem)
     out.start()
     vectors = vec_ref[...]
-    residual = dot_full(vectors, op_ref[...], ((1,), (1,))) - val_ref[...] * vectors
+    eigs = vectors.shape[0]
+    line = lax.broadcasted_iota(jnp.int32, (eigs, 1), 0)
+    values = jnp.zeros((eigs, 1), jnp.float32)
+    for k in range(eigs):
+        values = jnp.where(line == k, val_ref[k], values)
+    residual = dot_full(vectors, op_ref[...], ((1,), (1,))) - values * vectors
     res_ref[...] = residual
-    norm_ref[...] = jnp.sqrt(jnp.sum(residual * residual, axis=1, keepdims=True) + 1e-06)
+    squares = dot_full(jnp.ones((8, width), jnp.float32), residual * residual, ((1,), (1,)))
+    norm_ref[...] = jnp.sqrt(squares[0] + 1e-06)
     out.wait()
 
 
-def solve(core, own, other, vectors, values):
+def core_index():
+    return lax.axis_index("tm") & 1
+
+
+def solve(own, other, vectors, values, core_of=core_index):
     eigs, width = vectors.shape
     vmem = pl.BlockSpec(memory_space=pltpu.VMEM)
     square = pltpu.VMEM((width, width), jnp.float32)
-    operator, residual, norm = pl.pallas_call(
-        solve_kernel,
+    near = functools.partial(pltpu.with_memory_space_constraint, memory_space=pltpu.VMEM)
+    return pl.pallas_call(
+        functools.partial(solve_kernel, core_of),
         out_shape=(
             jax.ShapeDtypeStruct((width, width), jnp.float32),
             jax.ShapeDtypeStruct((eigs, width), jnp.float32),
-            jax.ShapeDtypeStruct((eigs, 1), jnp.float32),
+            jax.ShapeDtypeStruct((eigs,), jnp.float32),
         ),
-        in_specs=[pl.BlockSpec(memory_space=pltpu.SMEM), vmem, vmem, vmem, vmem],
+        in_specs=[vmem, vmem, vmem, pl.BlockSpec(memory_space=pltpu.SMEM)],
         out_specs=(pl.BlockSpec(memory_space=pl.ANY), vmem, vmem),
         scratch_shapes=[square] * 5
         + [pltpu.VMEM((width, 2 * width), jnp.float32), pltpu.SemaphoreType.DMA],
+        compiler_params=pltpu.CompilerParams(vmem_limit_bytes=16 * 2**20),
         name="solve",
-    )(core, own, other, vectors, values[:, None])
-    return operator, residual, norm[:, 0]
+    )(near(own), near(other), vectors, values)
+
+
+def project_kernel(chunk, modes_hbm, snaps_hbm, out, modes_vmem, snaps_vmem, total, mode_sem, snap_sem):
+    steps = modes_hbm.shape[0] // chunk
+
+    def copies(step):
+        lines = pl.ds(step * chunk, chunk)
+        return (
+            pltpu.make_async_copy(modes_hbm.at[lines], modes_vmem.at[lines], mode_sem.at[step]),
+            pltpu.make_async_copy(snaps_hbm.at[lines], snaps_vmem.at[lines], snap_sem.at[step]),
+        )
+
+    for step in range(steps):
+        for copy in copies(step):
+            copy.start()
+    total[...] = jnp.zeros_like(total)
+
+    def add(step, carry):
+        for copy in copies(step):
+            copy.wait()
+        lines = pl.ds(pl.multiple_of(step * chunk, chunk), chunk)
+        total[...] += lax.dot_general(
+            snaps_vmem[lines, :],
+            modes_vmem[lines, :],
+            (((0,), (0,)), ((), ())),
+            preferred_element_type=jnp.float32,
+        )
+        return carry
+
+    lax.fori_loop(0, steps, add, 0)
+    out[...] = total[...].T
+
+
+def project(modes, snapshots, chunk=2048):
+    width, cols = modes.shape[1], snapshots.shape[1]
+    steps = modes.shape[0] // chunk
+    far = functools.partial(pltpu.with_memory_space_constraint, memory_space=pltpu.HBM)
+    return pl.pallas_call(
+        functools.partial(project_kernel, chunk),
+        out_shape=jax.ShapeDtypeStruct((width, cols), jnp.float32),
+        in_specs=[pl.BlockSpec(memory_space=pltpu.HBM)] * 2,
+        out_specs=pl.BlockSpec(memory_space=pltpu.VMEM),
+        scratch_shapes=[
+            pltpu.VMEM(modes.shape, modes.dtype),
+            pltpu.VMEM(snapshots.shape, snapshots.dtype),
+            pltpu.VMEM((cols, width), jnp.float32),
+            pltpu.SemaphoreType.DMA((steps,)),
+            pltpu.SemaphoreType.DMA((steps,)),
+        ],
+        compiler_params=pltpu.CompilerParams(vmem_limit_bytes=40 * 2**20),
+        name="project",
+    )(far(modes), far(snapshots))
 
 
 def joint_groups():
@@ -174,7 +237,7 @@
     width = modes.shape[1]
     block_cols = snapshots.shape[1]
     rows = lax.axis_size("rows")
-    partial_value = jnp.einsum("mr,mt->rt", modes, snapshots, preferred_element_type=jnp.float32)
+    partial_value = project(modes, snapshots)
     lines = width // rows
     arrived = lax.all_to_all(
         partial_value.reshape(rows, lines, block_cols), "rows", 0, 0, tiled=True
@@ -191,9 +254,8 @@
     )
     swap = [(i, i ^ 1) for i in range(4 * rows)]
     other = lax.ppermute(gathered, axes, swap)
-    core = (lax.axis_index("tm") % 2).astype(jnp.int32).reshape(1)
     shape = (rows, 2, lines, block_cols)
-    return solve(core, gathered.reshape(shape), other.reshape(shape), eig_vectors, eig_values)
+    return solve(gathered.reshape(shape), other.reshape(shape), eig_vectors, eig_values)
 
 
 def solution(mesh):

time: 59.1 us -> 56.3 us (0.953); the launches traced: 60.1 us -> 56.1 us
  matrix products: 10.6 us -> 0 us
  Pallas kernels: 8.77 us -> 17.4 us
  local copies, waits for them, and re-layouts: 1.4 us -> 0.03 us
  other arithmetic: 1.34 us -> 0.04 us
  waiting for transfers between devices: 0.48 us -> 1.16 us
    dot_general x1 -> x0, matrix products: 10.6 us -> none  [body(): jnp.einsum('mr,mt->rt', modes, snapshots, preferred_element_type=jnp.floa...]
    pallas_call x1 -> x2, Pallas kernels: 8.77 us -> 17.4 us  [the longest x1 8.87 us: project(): pl.pallas_call(functools.partial(project_kernel, chunk), out_shape=jax.Sh...]
    pallas_call x1 -> x0, other arithmetic: 1.3 us -> none  [solve(): pl.pallas_call(solve_kernel, out_shape=(jax.ShapeDtypeStruct((width, widt...]
    unnamed x6 -> x4, local copies, waits for them, and re-layouts: 0.7 us -> 0.01 us
    ppermute x1, waiting for transfers between devices: 0.48 us -> 1.16 us  [body(): other = lax.ppermute(gathered, axes, swap)]
    broadcast_in_dim x1 -> x0, local copies, waits for them, and re-layouts: 0.68 us -> none  [solve(): values[:, None]]
  transfers between devices with their start and end apart: 1 -> 1, of which waited for: 1 -> 1; matrix products, arithmetic and copies ran while one was open for 1% -> 0% of each run, Pallas kernels for 0% -> 0%
where the time goes in v2:
time: 56.3 us; the launch traced here: 56.1 us
  blocking collectives  33.4 us (59%)
  Pallas kernels  17.4 us (31%)
  starting transfers between devices  3.44 us (6%)
  waiting for transfers between devices  1.16 us (2%)
  between operations  0.66 us (1%)
    all_to_all x1, blocking collectives, body(): lax.all_to_all(partial_value.reshape(rows, lines, block_cols), 'rows', 0,...  19.9 us
    all_to_all x1, blocking collectives, body(): lax.all_to_all(jnp.broadcast_to(own_lines[None], (2 * rows, lines, block_...  13.5 us
    pallas_call x1, Pallas kernels, project(): pl.pallas_call(functools.partial(project_kernel, chunk), out_shape=jax.Sh...  8.87 us
    pallas_call x1, Pallas kernels, solve(): pl.pallas_call(functools.partial(solve_kernel, core_of), out_shape=(jax.S...  8.5 us
    ppermute x1, starting transfers between devices, body(): other = lax.ppermute(gathered, axes, swap)  3.44 us
    ppermute x1, waiting for transfers between devices, body(): other = lax.ppermute(gathered, axes, swap)  1.16 us
  transfers between devices with their start and end apart: 1, of which 1 were waited for; matrix products, arithmetic and copies ran while one was open for 0% of the time, Pallas kernels for 0%

profile of v2, /device:TPU:1, one launch (start us, length us, event | category | flops | bytes accessed | tf_op | source)
XLA Modules:
  0.0 56.1 jit_solution(8159701417340754297)
XLA Ops:
  0.6 0.0 copy-start.1
  0.6 0.0 copy-start
  0.7 8.9 %project.1 = f32[256,128]{1,0:T(8,128)S(1)} custom-call(bf16[32768,256]{1,0:T(8,128)(2,1)} %modes_hbm.1, bf16[32768,128]{1,0:T(8,128)(2,1)} %snaps_hbm.1), custom_call_target="tpu_custom_call" | custom-call | tf_op jit(solution)/shard_map/project/pallas_call | solution.py:214
  9.5 19.9 %all_to_all.10 = f32[32,8,128]{2,1,0:T(8,128)S(1)} all-to-all(f32[32,8,128]{2,1,0:T(8,128)S(1)} %bitcast.4), channel_id=1, replica_groups=mesh['rows'=32,'tm'=4] {'rows'}, dimensions={0} | all-to-all | bytes 262144 | tf_op jit(solution)/shard_map/all_to_all | solution.py:242
  29.5 13.5 %all_to_all.11 = f32[64,8,128]{2,1,0:T(8,128)S(1)} all-to-all(f32[64,8,128]{2,1,0:T(8,128)S(1)} %broadcast_in_dim.2), channel_id=1, replica_groups={{0,2,4,6,8,10,12,14,16,18,20,22,24,26,28,30,32,34,36,38,40,42,44,46,48,..., dimensions={0} | all-to-all | bytes 524288 | tf_op jit(solution)/shard_map/all_to_all | solution.py:247
  43.0 3.4 %collective-permute-start = (f32[64,8,128]{2,1,0:T(8,128)S(1)}, f32[64,8,128]{2,1,0:T(8,128)S(1)}, u32[]{:S(2)}, u32[]{:S(2)}) collective-permute-start(f32[64,8,128]{2,1,0:T(8,128)S(1)} %all_to_all.11), channel_id=1, source_target_pairs={{0,1},{1,0},{2,3},{3,2},{4,5},{5,4},{6,7},{7,6},{8,9},{9,8},{10,11... | collective-permute-start | bytes 786440 | tf_op jit(solution)/shard_map/ppermute | solution.py:256
  46.5 1.2 %collective-permute-done = f32[64,8,128]{2,1,0:T(8,128)S(1)} collective-permute-done((f32[64,8,128]{2,1,0:T(8,128)S(1)}, f32[64,8,128]{2,1,0:T(8,128)S(1)}, u32[]{:S(2)}, u32[]{:S(2)}) %collective-permute-start) | collective-permute-done | bytes 262176 | tf_op jit(solution)/shard_map/ppermute | solution.py:256
  47.6 0.0 copy-done.1
  47.6 0.0 copy-done
  47.6 8.5 %solve.1 = (f32[256,256]{1,0:T(8,128)}, f32[3,256]{1,0:T(4,128)}, f32[3]{0:T(128)}) custom-call(f32[32,2,8,128]{3,2,1,0:T(8,128)S(1)} %bitcast.3, f32[32,2,8,128]{3,2,1,0:T(8,128)S(1)} %bitcast.5, f32[3,256]{1,0:T(4,128)S(1)} %copy-done, f32[3]{0:T(128)S(1)} %copy-done.1), custom_call_target="tpu_custom_call" | custom-call | tf_op jit(solution)/shard_map/solve/pallas_call | solution.py:163
  (2 shorter events, 0.1 us)
Async XLA Ops:
  0.6 47.0 %copy-start.1 = (f32[3]{0:T(128)S(1)}, f32[3]{0:T(128)}, u32[]{:S(2)}) copy-start(f32[3]{0:T(128)} %val_ref.1) | copy-start | bytes 40
  0.6 47.0 %copy-start = (f32[3,256]{1,0:T(4,128)S(1)}, f32[3,256]{1,0:T(4,128)}, u32[]{:S(2)}) copy-start(f32[3,256]{1,0:T(4,128)} %vec_ref.1) | copy-start | bytes 9220
  43.0 4.6 %collective-permute-start = (f32[64,8,128]{2,1,0:T(8,128)S(1)}, f32[64,8,128]{2,1,0:T(8,128)S(1)}, u32[]{:S(2)}, u32[]{:S(2)}) collective-permute-start(f32[64,8,128]{2,1,0:T(8,128)S(1)} %all_to_all.11), channel_id=1, source_target_pairs={{0,1},{1,0},{2,3},{3,2},{4,5},{5,4},{6,7},{7,6},{8,9},{9,8},{10,11... | collective-permute-start | bytes 786440 | tf_op jit(solution)/shard_map/ppermute | solution.py:256

commit v3 on v2

--- a/solution.py
+++ b/solution.py
@@ -1,4 +1,5 @@
 import functools
+import math
 
 import jax
 import jax.numpy as jnp
@@ -32,6 +33,13 @@
         precision=lax.Precision.HIGHEST,
         preferred_element_type=jnp.float32,
     )
+
+
+def bound_for(doublings):
+    t = RESIDUAL_FLOOR
+    for _ in range(doublings + 1):
+        t = math.sqrt((t + 1.0) / 2.0)
+    return (t + 1.0) / (t - 1.0)
 
 
 def eliminate(gram_ref, work, width):
@@ -51,115 +59,171 @@
     lax.fori_loop(0, width, step, 0)
 
 
-def solve_kernel(core_of, own_ref, other_ref, vec_ref, val_ref, op_out, res_ref, norm_ref,
-                 gram_ref, cross_ref, r_ref, x_ref, op_ref, work, sem):
+def core_index():
+    return lax.axis_index("tm") & 1
+
+
+def block_of(ref, half):
+    return ref[:, half].reshape(-1, ref.shape[-1])
+
+
+def half_sums(blocks, drop_last):
+    cols = blocks[0].shape[1]
+    column = lax.broadcasted_iota(jnp.int32, (1, cols), 1)
+    inner = column < cols - 1
+    leads = jnp.concatenate(
+        [blocks[0], jnp.where(jnp.logical_or(inner, jnp.logical_not(drop_last)), blocks[1], 0.0)],
+        axis=1,
+    )
+    starts = jnp.concatenate([jnp.where(inner, block, 0.0) for block in blocks], axis=1)
+    nexts = jnp.concatenate([pltpu.roll(block, cols - 1, 1) for block in blocks], axis=1)
+    gram = dot_full(leads, leads, ((1,), (1,)))
+    cross = dot_full(nexts, starts, ((1,), (1,)))
+    return gram, cross
+
+
+def own_kernel(core_of, own_ref, gram_ref, cross_ref):
+    blocks = [block_of(own_ref, 0), block_of(own_ref, 1)]
+    gram, cross = half_sums(blocks, core_of() == 1)
+    gram_ref[...] = gram
+    cross_ref[...] = cross
+
+
+def near(array):
+    return pltpu.with_memory_space_constraint(array, pltpu.VMEM)
+
+
+def own_sums(own, width, core_of=core_index):
+    vmem = pl.BlockSpec(memory_space=pltpu.VMEM)
+    square = jax.ShapeDtypeStruct((width, width), jnp.float32)
+    return pl.pallas_call(
+        functools.partial(own_kernel, core_of),
+        out_shape=(square, square),
+        in_specs=[vmem],
+        out_specs=(vmem, vmem),
+        compiler_params=pltpu.CompilerParams(vmem_limit_bytes=16 * 2**20),
+        cost_estimate=pl.CostEstimate(
+            flops=24 * width**3, bytes_accessed=12 * width * width, transcendentals=0
+        ),
+        name="own_sums",
+    )(near(own))
+
+
+def solve_kernel(core_of, own_ref, other_ref, gram_own_ref, cross_own_ref, vec_ref, val_ref,
+                 op_out, res_out, norm_out,
+                 gram_ref, cross_ref, r_ref, x_ref, op_ref, work, res_ref, norm_ref, sems):
     width = gram_ref.shape[0]
-    first = core_of() == 0
-    blocks = []
-    for half in range(2):
-        own = own_ref[:, half].reshape(width, 128)
-        other = other_ref[:, half].reshape(width, 128)
-        blocks.append(jnp.where(first, own, other))
-        blocks.append(jnp.where(first, other, own))
-    series = jnp.concatenate(blocks, axis=1)
-    total = series.shape[1]
-    scale = 1.0 / (total - 1)
-    column = lax.broadcasted_iota(jnp.int32, (1, total), 1)
-    lead = jnp.where(column < total - 1, series, 0.0)
-    trail = pltpu.roll(series, total - 1, 1)
-    both = dot_full(jnp.concatenate([lead, trail], axis=0), lead, ((1,), (1,)))
+    core = core_of()
+    first = core == 0
+    own = [block_of(own_ref, half) for half in range(2)]
+    other = [block_of(other_ref, half) for half in range(2)]
+    cols = own[0].shape[1]
+    scale = 1.0 / (4 * cols - 1)
     eye = (
         lax.broadcasted_iota(jnp.int32, (width, width), 0)
         == lax.broadcasted_iota(jnp.int32, (width, width), 1)
     ).astype(jnp.float32)
-    gram = both[:width] * scale + eye
-    cross = both[width:] * scale
+    gram_other, cross_other = half_sums(other, first)
+    gram = (gram_own_ref[...] + gram_other) * scale + eye
     gram_ref[...] = gram
-    cross_ref[...] = cross
-
     gram_pieces = pieces(gram)
     square = dot3(gram_pieces, gram_pieces)
-    top = jnp.max(jnp.sum(jnp.abs(square), axis=0, keepdims=True))
-    top = jnp.maximum(jnp.sqrt(jnp.full((8, 128), top, jnp.float32)) * 1.001, 1.5)
-    bound = jnp.max(top)
-
-    @pl.when(bound <= LARGEST_FAST)
+
+    lane = lax.broadcasted_iota(jnp.int32, (1, cols), 1)
+    series = []
+    for half in range(2):
+        series.append(jnp.where(first, own[half], other[half]))
+        series.append(jnp.where(first, other[half], own[half]))
+    ends = jnp.zeros_like(series[0])
+    begins = jnp.zeros_like(series[0])
+    for k in range(3):
+        ends = jnp.where(lane == k, pltpu.roll(series[k], k + 1, 1), ends)
+        begin = series[k + 1] if k == 0 else pltpu.roll(series[k + 1], k, 1)
+        begins = jnp.where(lane == k, begin, begins)
+    edges = dot_full(begins, ends, ((1,), (1,)))
+    cross_ref[...] = (cross_own_ref[...] + cross_other + edges) * scale
+
+    vectors = vec_ref[...]
+    eigs = vectors.shape[0]
+    on_diagonal = (
+        lax.broadcasted_iota(jnp.int32, (eigs, eigs), 0)
+        == lax.broadcasted_iota(jnp.int32, (eigs, eigs), 1)
+    )
+    values = jnp.sum(jnp.where(on_diagonal, val_ref[...][None, :], 0.0), axis=1, keepdims=True)
+
+    top = jnp.max(jnp.sum(jnp.abs(square), axis=0, keepdims=True), axis=1, keepdims=True)
+    bound_squared = top[0, 0]
+    top = jnp.maximum(jnp.sqrt(top) * 1.001, 1.5)
+    doublings = jnp.int32(0)
+    for k in range(1, 8):
+        doublings += (bound_squared > (bound_for(k) / 1.001) ** 2).astype(jnp.int32)
+
+    @pl.when(bound_squared <= LARGEST_FAST**2)
     def _():
         alpha = 2.0 / (top + 1.0)
         t1 = (top + 1.0) / (top - 1.0)
         t2 = 2.0 * t1 * t1 - 1.0
-        inv2 = 1.0 / t2
-        a = alpha[:1, :1]
-        i2 = inv2[:1, :1]
+        i2 = 1.0 / t2
         c = 1.0 + i2
-        r_ref[...] = c * (eye - (2.0 * a) * gram_ref[...] + (a * a) * square) - i2 * eye
-        x_ref[...] = (c * a) * (2.0 * eye - a * gram_ref[...])
-
-        def more(state):
-            return jnp.max(2.0 * state * state - 1.0) < RESIDUAL_FLOOR
-
-        def double(t):
+        r_ref[...] = c * (eye - (2.0 * alpha) * gram_ref[...] + (alpha * alpha) * square) - i2 * eye
+        x_ref[...] = (c * alpha) * (2.0 * eye - alpha * gram_ref[...])
+
+        def double(_, t):
             t = 2.0 * t * t - 1.0
-            it = (1.0 / t)[:1, :1]
-            r = r_ref[...]
+            it = 1.0 / t
             x = x_ref[...]
-            rp = pieces(r)
+            rp = pieces(r_ref[...])
             x_ref[...] = (1.0 + it) * (x + dot3(pieces(x), rp))
             r_ref[...] = (1.0 + it) * dot3(rp, rp) - it * eye
             return t
 
-        t = lax.while_loop(more, double, t2)
+        t = lax.fori_loop(0, doublings, double, t2)
         t = 2.0 * t * t - 1.0
-        it = (1.0 / t)[:1, :1]
         x = x_ref[...]
-        x = (1.0 + it) * (x + dot3(pieces(x), pieces(r_ref[...])))
+        x = (1.0 + 1.0 / t) * (x + dot3(pieces(x), pieces(r_ref[...])))
+        x_ref[...] = x
         xp = pieces(x)
-        x_ref[...] = x
-
-        def refine(guess):
+
+        def refine(guess, xp):
             rest = cross_ref[...] - dot_full(guess, gram_ref[...])
             return guess + dot3(pieces(rest), xp)
 
-        last = 1.0 + (1.0 / (2.0 * t * t - 1.0))[:1, :1]
-        guess = dot3(pieces(cross_ref[...]), xp)
-        op_ref[...] = last * refine(guess)
-
-        @pl.when(bound > 32.0)
-        def _():
-            for _ in range(3):
-                op_ref[...] = refine(op_ref[...])
-
-    @pl.when(bound > LARGEST_FAST)
+        last = 1.0 + 1.0 / (2.0 * t * t - 1.0)
+        op_ref[...] = last * refine(dot3(pieces(cross_ref[...]), xp), xp)
+
+        def again(_, carry):
+            op_ref[...] = refine(op_ref[...], pieces(x_ref[...]))
+            return carry
+
+        lax.fori_loop(0, jnp.where(bound_squared > 32.0**2, 3, 0), again, 0)
+
+    @pl.when(bound_squared > LARGEST_FAST**2)
     def _():
         work[:, :width] = gram_ref[...]
         work[:, width:] = cross_ref[...].T
         eliminate(gram_ref, work, width)
         op_ref[...] = work[:, width:].T
 
-    out = pltpu.make_async_copy(op_ref, op_out, sem)
+    out = pltpu.make_async_copy(op_ref, op_out, sems.at[0])
     out.start()
-    vectors = vec_ref[...]
-    eigs = vectors.shape[0]
-    line = lax.broadcasted_iota(jnp.int32, (eigs, 1), 0)
-    values = jnp.zeros((eigs, 1), jnp.float32)
-    for k in range(eigs):
-        values = jnp.where(line == k, val_ref[k], values)
     residual = dot_full(vectors, op_ref[...], ((1,), (1,))) - values * vectors
     res_ref[...] = residual
+    res = pltpu.make_async_copy(res_ref, res_out, sems.at[1])
+    res.start()
     squares = dot_full(jnp.ones((8, width), jnp.float32), residual * residual, ((1,), (1,)))
     norm_ref[...] = jnp.sqrt(squares[0] + 1e-06)
+    norm = pltpu.make_async_copy(norm_ref, norm_out, sems.at[2])
+    norm.start()
     out.wait()
-
-
-def core_index():
-    return lax.axis_index("tm") & 1
-
-
-def solve(own, other, vectors, values, core_of=core_index):
+    res.wait()
+    norm.wait()
+
+
+def solve(own, other, gram_own, cross_own, vectors, values, core_of=core_index):
     eigs, width = vectors.shape
     vmem = pl.BlockSpec(memory_space=pltpu.VMEM)
+    hbm = pl.BlockSpec(memory_space=pltpu.HBM)
     square = pltpu.VMEM((width, width), jnp.float32)
-    near = functools.partial(pltpu.with_memory_space_constraint, memory_space=pltpu.VMEM)
     return pl.pallas_call(
         functools.partial(solve_kernel, core_of),
         out_shape=(
@@ -167,13 +231,18 @@
             jax.ShapeDtypeStruct((eigs, width), jnp.float32),
             jax.ShapeDtypeStruct((eigs,), jnp.float32),
         ),
-        in_specs=[vmem, vmem, vmem, pl.BlockSpec(memory_space=pltpu.SMEM)],
-        out_specs=(pl.BlockSpec(memory_space=pl.ANY), vmem, vmem),
+        in_specs=[vmem] * 6,
+        out_specs=(hbm, hbm, hbm),
         scratch_shapes=[square] * 5
-        + [pltpu.VMEM((width, 2 * width), jnp.float32), pltpu.SemaphoreType.DMA],
+        + [
+            pltpu.VMEM((width, 2 * width), jnp.float32),
+            pltpu.VMEM((eigs, width), jnp.float32),
+            pltpu.VMEM((eigs,), jnp.float32),
+            pltpu.SemaphoreType.DMA((3,)),
+        ],
         compiler_params=pltpu.CompilerParams(vmem_limit_bytes=16 * 2**20),
         name="solve",
-    )(near(own), near(other), vectors, values)
+    )(*map(near, (own, other, gram_own, cross_own, vectors, values)))
 
 
 def project_kernel(chunk, modes_hbm, snaps_hbm, out, modes_vmem, snaps_vmem, total, mode_sem, snap_sem):
@@ -255,7 +324,9 @@
     swap = [(i, i ^ 1) for i in range(4 * rows)]
     other = lax.ppermute(gathered, axes, swap)
     shape = (rows, 2, lines, block_cols)
-    return solve(gathered.reshape(shape), other.reshape(shape), eig_vectors, eig_values)
+    own, other = gathered.reshape(shape), other.reshape(shape)
+    gram_own, cross_own = own_sums(own, width)
+    return solve(own, other, gram_own, cross_own, eig_vectors, eig_values)
 
 
 def solution(mesh):

time: 56.3 us -> 53.6 us (0.952); the launches traced: 56.1 us -> 54.5 us
  Pallas kernels: 17.4 us -> 16.4 us
  waiting for transfers between devices: 1.16 us -> 0.52 us
    pallas_call x1, Pallas kernels: 8.5 us -> 6.86 us  [solve(): pl.pallas_call(functools.partial(solve_kernel, core_of), out_shape=(jax.S...]
    ppermute x1, waiting for transfers between devices: 1.16 us -> 0.52 us  [body(): other = lax.ppermute(gathered, axes, swap)]
    pallas_call x0 -> x1, Pallas kernels: none -> 0.64 us  [own_sums(): pl.pallas_call(functools.partial(own_kernel, core_of), out_shape=(square,...]
  transfers between devices with their start and end apart: 1 -> 1, of which waited for: 1 -> 1; matrix products, arithmetic and copies ran while one was open for 0% -> 0% of each run, Pallas kernels for 0% -> 1%
where the time goes in v3:
time: 53.6 us; the launch traced here: 54.5 us
  blocking collectives  33.4 us (62%)
  Pallas kernels  16.4 us (31%)
  starting transfers between devices  3.44 us (6%)
  between operations  0.67 us (1%)
    all_to_all x1, blocking collectives, body(): lax.all_to_all(partial_value.reshape(rows, lines, block_cols), 'rows', 0,...  19.9 us
    all_to_all x1, blocking collectives, body(): lax.all_to_all(jnp.broadcast_to(own_lines[None], (2 * rows, lines, block_...  13.5 us
    pallas_call x1, Pallas kernels, project(): pl.pallas_call(functools.partial(project_kernel, chunk), out_shape=jax.Sh...  8.87 us
    pallas_call x1, Pallas kernels, solve(): pl.pallas_call(functools.partial(solve_kernel, core_of), out_shape=(jax.S...  6.86 us
    ppermute x1, starting transfers between devices, body(): other = lax.ppermute(gathered, axes, swap)  3.44 us
  transfers between devices with their start and end apart: 1, of which 1 were waited for; matrix products, arithmetic and copies ran while one was open for 0% of the time, Pallas kernels for 1%

profile of v3, /device:TPU:1, one launch (start us, length us, event | category | flops | bytes accessed | tf_op | source)
XLA Modules:
  0.0 54.5 jit_solution(8375050601043290733)
XLA Ops:
  0.6 0.0 copy-start.1
  0.6 0.0 copy-start
  0.7 8.9 %project.1 = f32[256,128]{1,0:T(8,128)S(1)} custom-call(bf16[32768,256]{1,0:T(8,128)(2,1)} %modes_hbm.1, bf16[32768,128]{1,0:T(8,128)(2,1)} %snaps_hbm.1), custom_call_target="tpu_custom_call" | custom-call | tf_op jit(solution)/shard_map/project/pallas_call | solution.py:283
  9.5 19.9 %all_to_all.10 = f32[32,8,128]{2,1,0:T(8,128)S(1)} all-to-all(f32[32,8,128]{2,1,0:T(8,128)S(1)} %bitcast.5), channel_id=1, replica_groups=mesh['rows'=32,'tm'=4] {'rows'}, dimensions={0} | all-to-all | bytes 262144 | tf_op jit(solution)/shard_map/all_to_all | solution.py:311
  29.5 13.5 %all_to_all.11 = f32[64,8,128]{2,1,0:T(8,128)S(1)} all-to-all(f32[64,8,128]{2,1,0:T(8,128)S(1)} %broadcast_in_dim.2), channel_id=1, replica_groups={{0,2,4,6,8,10,12,14,16,18,20,22,24,26,28,30,32,34,36,38,40,42,44,46,48,..., dimensions={0} | all-to-all | bytes 524288 | tf_op jit(solution)/shard_map/all_to_all | solution.py:316
  43.0 3.4 %collective-permute-start = (f32[64,8,128]{2,1,0:T(8,128)S(1)}, f32[64,8,128]{2,1,0:T(8,128)S(1)}, u32[]{:S(2)}, u32[]{:S(2)}) collective-permute-start(f32[64,8,128]{2,1,0:T(8,128)S(1)} %all_to_all.11), channel_id=1, source_target_pairs={{0,1},{1,0},{2,3},{3,2},{4,5},{5,4},{6,7},{7,6},{8,9},{9,8},{10,11... | collective-permute-start | bytes 786440 | tf_op jit(solution)/shard_map/ppermute | solution.py:325
  46.5 0.6 %own_sums.1 = (f32[256,256]{1,0:T(8,128)S(1)}, f32[256,256]{1,0:T(8,128)S(1)}) custom-call(f32[32,2,8,128]{3,2,1,0:T(8,128)S(1)} %bitcast.3), custom_call_target="tpu_custom_call" | custom-call | flops 402653184 | bytes 786432 | tf_op jit(solution)/shard_map/own_sums/pallas_call | solution.py:99
  47.1 0.5 collective-permute-done
  47.6 0.0 copy-done.1
  47.6 0.0 copy-done
  47.6 6.9 %solve.1 = (f32[256,256]{1,0:T(8,128)}, f32[3,256]{1,0:T(4,128)}, f32[3]{0:T(128)}) custom-call(f32[32,2,8,128]{3,2,1,0:T(8,128)S(1)} %bitcast.4, f32[32,2,8,128]{3,2,1,0:T(8,128)S(1)} %bitcast.6, f32[256,256]{1,0:T(8,128)S(1)} %get-tuple-element.5.gram_own_ref, f32[256,256]{1,0:T(8,128)S(1)} %get-tuple-element.6.cross_own_ref, f32[3,256]{1,0:T(4,128)S(1)} %copy-done, ...), custom_call_target="tpu_custom_call" | custom-call | tf_op jit(solution)/shard_map/solve/pallas_call | solution.py:227
  (2 shorter events, 0.1 us)
Async XLA Ops:
  0.6 47.0 %copy-start.1 = (f32[3]{0:T(128)S(1)}, f32[3]{0:T(128)}, u32[]{:S(2)}) copy-start(f32[3]{0:T(128)} %val_ref.1) | copy-start | bytes 40
  0.6 47.0 %copy-start = (f32[3,256]{1,0:T(4,128)S(1)}, f32[3,256]{1,0:T(4,128)}, u32[]{:S(2)}) copy-start(f32[3,256]{1,0:T(4,128)} %vec_ref.1) | copy-start | bytes 9220
  43.0 4.6 %collective-permute-start = (f32[64,8,128]{2,1,0:T(8,128)S(1)}, f32[64,8,128]{2,1,0:T(8,128)S(1)}, u32[]{:S(2)}, u32[]{:S(2)}) collective-permute-start(f32[64,8,128]{2,1,0:T(8,128)S(1)} %all_to_all.11), channel_id=1, source_target_pairs={{0,1},{1,0},{2,3},{3,2},{4,5},{5,4},{6,7},{7,6},{8,9},{9,8},{10,11... | collective-permute-start | bytes 786440 | tf_op jit(solution)/shard_map/ppermute | solution.py:325

commit v4 on v3

--- a/solution.py
+++ b/solution.py
@@ -10,6 +10,8 @@
 
 LARGEST_FAST = 2048.0
 RESIDUAL_FLOOR = 224.0
+PLAIN = ((1,), (0,))
+ACROSS = ((1,), (1,))
 
 
 def pieces(array):
@@ -18,14 +20,17 @@
     return high, low
 
 
-def dot3(left, right):
+def dot3(left, right, contract=PLAIN):
     left_high, left_low = left
     right_high, right_low = right
-    mm = functools.partial(jnp.dot, preferred_element_type=jnp.float32)
+
+    def mm(a, b):
+        return lax.dot_general(a, b, (contract, ((), ())), preferred_element_type=jnp.float32)
+
     return mm(left_high, right_high) + (mm(left_high, right_low) + mm(left_low, right_high))
 
 
-def dot_full(left, right, contract=((1,), (0,))):
+def dot_full(left, right, contract=PLAIN):
     return lax.dot_general(
         left,
         right,
@@ -77,8 +82,8 @@
     )
     starts = jnp.concatenate([jnp.where(inner, block, 0.0) for block in blocks], axis=1)
     nexts = jnp.concatenate([pltpu.roll(block, cols - 1, 1) for block in blocks], axis=1)
-    gram = dot_full(leads, leads, ((1,), (1,)))
-    cross = dot_full(nexts, starts, ((1,), (1,)))
+    gram = dot_full(leads, leads, ACROSS)
+    cross = dot_full(nexts, starts, ACROSS)
     return gram, cross
 
 
@@ -111,7 +116,7 @@
 
 def solve_kernel(core_of, own_ref, other_ref, gram_own_ref, cross_own_ref, vec_ref, val_ref,
                  op_out, res_out, norm_out,
-                 gram_ref, cross_ref, r_ref, x_ref, op_ref, work, res_ref, norm_ref, sems):
+                 gram_ref, cross_ref, r_ref, x_ref, op_ref, work, seen_ref, res_ref, norm_ref, sems):
     width = gram_ref.shape[0]
     core = core_of()
     first = core == 0
@@ -140,7 +145,7 @@
         ends = jnp.where(lane == k, pltpu.roll(series[k], k + 1, 1), ends)
         begin = series[k + 1] if k == 0 else pltpu.roll(series[k + 1], k, 1)
         begins = jnp.where(lane == k, begin, begins)
-    edges = dot_full(begins, ends, ((1,), (1,)))
+    edges = dot_full(begins, ends, ACROSS)
     cross_ref[...] = (cross_own_ref[...] + cross_other + edges) * scale
 
     vectors = vec_ref[...]
@@ -184,18 +189,23 @@
         x_ref[...] = x
         xp = pieces(x)
 
-        def refine(guess, xp):
+        guess = dot3(pieces(cross_ref[...]), xp)
+        seen = dot_full(vectors, guess, ACROSS)
+        mixed = dot3(pieces(vectors), xp, ACROSS)
+        rest = pieces(cross_ref[...] - dot_full(guess, gram_ref[...]))
+        last = 1.0 + 1.0 / (2.0 * t * t - 1.0)
+        op_ref[...] = last * (guess + dot3(rest, xp))
+        seen_ref[...] = last * (seen + dot3(pieces(mixed), rest, ACROSS))
+
+    @pl.when(jnp.logical_and(bound_squared > 32.0**2, bound_squared <= LARGEST_FAST**2))
+    def _():
+        def again(_, carry):
+            guess = op_ref[...]
             rest = cross_ref[...] - dot_full(guess, gram_ref[...])
-            return guess + dot3(pieces(rest), xp)
-
-        last = 1.0 + 1.0 / (2.0 * t * t - 1.0)
-        op_ref[...] = last * refine(dot3(pieces(cross_ref[...]), xp), xp)
-
-        def again(_, carry):
-            op_ref[...] = refine(op_ref[...], pieces(x_ref[...]))
+            op_ref[...] = guess + dot3(pieces(rest), pieces(x_ref[...]))
             return carry
 
-        lax.fori_loop(0, jnp.where(bound_squared > 32.0**2, 3, 0), again, 0)
+        lax.fori_loop(0, 3, again, 0)
 
     @pl.when(bound_squared > LARGEST_FAST**2)
     def _():
@@ -206,12 +216,18 @@
 
     out = pltpu.make_async_copy(op_ref, op_out, sems.at[0])
     out.start()
-    residual = dot_full(vectors, op_ref[...], ((1,), (1,))) - values * vectors
+
+    @pl.when(bound_squared > 32.0**2)
+    def _():
+        seen_ref[...] = dot_full(vectors, op_ref[...], ACROSS)
+
+    residual = seen_ref[...] - values * vectors
     res_ref[...] = residual
     res = pltpu.make_async_copy(res_ref, res_out, sems.at[1])
     res.start()
-    squares = dot_full(jnp.ones((8, width), jnp.float32), residual * residual, ((1,), (1,)))
-    norm_ref[...] = jnp.sqrt(squares[0] + 1e-06)
+    sums = jnp.sum(residual * residual, axis=1, keepdims=True)
+    sums = jnp.sum(jnp.where(on_diagonal, sums, 0.0), axis=0)
+    norm_ref[...] = jnp.sqrt(sums + 1e-06)
     norm = pltpu.make_async_copy(norm_ref, norm_out, sems.at[2])
     norm.start()
     out.wait()
@@ -237,6 +253,7 @@
         + [
             pltpu.VMEM((width, 2 * width), jnp.float32),
             pltpu.VMEM((eigs, width), jnp.float32),
+            pltpu.VMEM((eigs, width), jnp.float32),
             pltpu.VMEM((eigs,), jnp.float32),
             pltpu.SemaphoreType.DMA((3,)),
         ],
@@ -247,38 +264,46 @@
 
 def project_kernel(chunk, modes_hbm, snaps_hbm, out, modes_vmem, snaps_vmem, total, mode_sem, snap_sem):
     steps = modes_hbm.shape[0] // chunk
-
-    def copies(step):
-        lines = pl.ds(step * chunk, chunk)
+    tail = chunk // 2
+
+    def copies(step, start, size):
+        lines = pl.ds(start, size)
         return (
             pltpu.make_async_copy(modes_hbm.at[lines], modes_vmem.at[lines], mode_sem.at[step]),
             pltpu.make_async_copy(snaps_hbm.at[lines], snaps_vmem.at[lines], snap_sem.at[step]),
         )
 
-    for step in range(steps):
-        for copy in copies(step):
+    pieces_of = [(step, step * chunk, chunk) for step in range(steps - 1)]
+    pieces_of += [(steps - 1 + k, (steps - 1) * chunk + k * tail, tail) for k in range(2)]
+    for piece in pieces_of:
+        for copy in copies(*piece):
             copy.start()
-    total[...] = jnp.zeros_like(total)
-
-    def add(step, carry):
-        for copy in copies(step):
+
+    def product(step, start, size):
+        for copy in copies(step, start, size):
             copy.wait()
-        lines = pl.ds(pl.multiple_of(step * chunk, chunk), chunk)
-        total[...] += lax.dot_general(
+        lines = pl.ds(start, size)
+        return lax.dot_general(
             snaps_vmem[lines, :],
             modes_vmem[lines, :],
             (((0,), (0,)), ((), ())),
             preferred_element_type=jnp.float32,
         )
+
+    total[...] = product(0, 0, chunk)
+
+    def add(step, carry):
+        total[...] += product(step, pl.multiple_of(step * chunk, chunk), chunk)
         return carry
 
-    lax.fori_loop(0, steps, add, 0)
-    out[...] = total[...].T
+    lax.fori_loop(1, steps - 1, add, 0)
+    total[...] += product(*pieces_of[-2])
+    out[...] = (total[...] + product(*pieces_of[-1])).T
 
 
 def project(modes, snapshots, chunk=2048):
     width, cols = modes.shape[1], snapshots.shape[1]
-    steps = modes.shape[0] // chunk
+    steps = modes.shape[0] // chunk + 1
     far = functools.partial(pltpu.with_memory_space_constraint, memory_space=pltpu.HBM)
     return pl.pallas_call(
         functools.partial(project_kernel, chunk),

time: 53.6 us -> 55.1 us (1.028); the launches traced: 54.5 us -> 54.9 us
  no operation moved by 1% of the time
where the time goes in v4:
time: 55.1 us; the launch traced here: 54.9 us
  blocking collectives  33.4 us (61%)
  Pallas kernels  16.7 us (30%)
  starting transfers between devices  3.44 us (6%)
  between operations  0.67 us (1%)
    all_to_all x1, blocking collectives, body(): lax.all_to_all(partial_value.reshape(rows, lines, block_cols), 'rows', 0,...  20 us
    all_to_all x1, blocking collectives, body(): lax.all_to_all(jnp.broadcast_to(own_lines[None], (2 * rows, lines, block_...  13.5 us
    pallas_call x1, Pallas kernels, project(): pl.pallas_call(functools.partial(project_kernel, chunk), out_shape=jax.Sh...  9.05 us
    pallas_call x1, Pallas kernels, solve(): pl.pallas_call(functools.partial(solve_kernel, core_of), out_shape=(jax.S...  7.05 us
    ppermute x1, starting transfers between devices, body(): other = lax.ppermute(gathered, axes, swap)  3.44 us
  transfers between devices with their start and end apart: 1, of which 1 were waited for; matrix products, arithmetic and copies ran while one was open for 0% of the time, Pallas kernels for 1%

profile of v4, /device:TPU:1, one launch (start us, length us, event | category | flops | bytes accessed | tf_op | source)
XLA Modules:
  0.0 54.9 jit_solution(3461724351035693003)
XLA Ops:
  0.6 0.0 copy-start.1
  0.6 0.0 copy-start
  0.7 9.0 %project.1 = f32[256,128]{1,0:T(8,128)S(1)} custom-call(bf16[32768,256]{1,0:T(8,128)(2,1)} %modes_hbm.1, bf16[32768,128]{1,0:T(8,128)(2,1)} %snaps_hbm.1), custom_call_target="tpu_custom_call" | custom-call | tf_op jit(solution)/shard_map/project/pallas_call | solution.py:308
  9.7 20.0 %all_to_all.10 = f32[32,8,128]{2,1,0:T(8,128)S(1)} all-to-all(f32[32,8,128]{2,1,0:T(8,128)S(1)} %bitcast.5), channel_id=1, replica_groups=mesh['rows'=32,'tm'=4] {'rows'}, dimensions={0} | all-to-all | bytes 262144 | tf_op jit(solution)/shard_map/all_to_all | solution.py:336
  29.7 13.5 %all_to_all.11 = f32[64,8,128]{2,1,0:T(8,128)S(1)} all-to-all(f32[64,8,128]{2,1,0:T(8,128)S(1)} %broadcast_in_dim.2), channel_id=1, replica_groups={{0,2,4,6,8,10,12,14,16,18,20,22,24,26,28,30,32,34,36,38,40,42,44,46,48,..., dimensions={0} | all-to-all | bytes 524288 | tf_op jit(solution)/shard_map/all_to_all | solution.py:341
  43.2 3.4 %collective-permute-start = (f32[64,8,128]{2,1,0:T(8,128)S(1)}, f32[64,8,128]{2,1,0:T(8,128)S(1)}, u32[]{:S(2)}, u32[]{:S(2)}) collective-permute-start(f32[64,8,128]{2,1,0:T(8,128)S(1)} %all_to_all.11), channel_id=1, source_target_pairs={{0,1},{1,0},{2,3},{3,2},{4,5},{5,4},{6,7},{7,6},{8,9},{9,8},{10,11... | collective-permute-start | bytes 786440 | tf_op jit(solution)/shard_map/ppermute | solution.py:350
  46.6 0.6 %own_sums.1 = (f32[256,256]{1,0:T(8,128)S(1)}, f32[256,256]{1,0:T(8,128)S(1)}) custom-call(f32[32,2,8,128]{3,2,1,0:T(8,128)S(1)} %bitcast.3), custom_call_target="tpu_custom_call" | custom-call | flops 402653184 | bytes 786432 | tf_op jit(solution)/shard_map/own_sums/pallas_call | solution.py:104
  47.3 0.5 collective-permute-done
  47.8 0.0 copy-done.1
  47.8 0.0 copy-done
  47.8 7.1 %solve.1 = (f32[256,256]{1,0:T(8,128)}, f32[3,256]{1,0:T(4,128)}, f32[3]{0:T(128)}) custom-call(f32[32,2,8,128]{3,2,1,0:T(8,128)S(1)} %bitcast.4, f32[32,2,8,128]{3,2,1,0:T(8,128)S(1)} %bitcast.6, f32[256,256]{1,0:T(8,128)S(1)} %get-tuple-element.5.gram_own_ref, f32[256,256]{1,0:T(8,128)S(1)} %get-tuple-element.6.cross_own_ref, f32[3,256]{1,0:T(4,128)S(1)} %copy-done, ...), custom_call_target="tpu_custom_call" | custom-call | tf_op jit(solution)/shard_map/solve/pallas_call | solution.py:243
  (2 shorter events, 0.1 us)
Async XLA Ops:
  0.6 47.2 %copy-start.1 = (f32[3]{0:T(128)S(1)}, f32[3]{0:T(128)}, u32[]{:S(2)}) copy-start(f32[3]{0:T(128)} %val_ref.1) | copy-start | bytes 40
  0.6 47.2 %copy-start = (f32[3,256]{1,0:T(4,128)S(1)}, f32[3,256]{1,0:T(4,128)}, u32[]{:S(2)}) copy-start(f32[3,256]{1,0:T(4,128)} %vec_ref.1) | copy-start | bytes 9220
  43.2 4.6 %collective-permute-start = (f32[64,8,128]{2,1,0:T(8,128)S(1)}, f32[64,8,128]{2,1,0:T(8,128)S(1)}, u32[]{:S(2)}, u32[]{:S(2)}) collective-permute-start(f32[64,8,128]{2,1,0:T(8,128)S(1)} %all_to_all.11), channel_id=1, source_target_pairs={{0,1},{1,0},{2,3},{3,2},{4,5},{5,4},{6,7},{7,6},{8,9},{9,8},{10,11... | collective-permute-start | bytes 786440 | tf_op jit(solution)/shard_map/ppermute | solution.py:350

commit v5 on v3

--- a/solution.py
+++ b/solution.py
@@ -9,7 +9,9 @@
 from jax.sharding import PartitionSpec as P
 
 LARGEST_FAST = 2048.0
-RESIDUAL_FLOOR = 224.0
+RESIDUAL_FLOOR = 150.0
+PLAIN = ((1,), (0,))
+ACROSS = ((1,), (1,))
 
 
 def pieces(array):
@@ -18,14 +20,17 @@
     return high, low
 
 
-def dot3(left, right):
+def dot3(left, right, contract=PLAIN):
     left_high, left_low = left
     right_high, right_low = right
-    mm = functools.partial(jnp.dot, preferred_element_type=jnp.float32)
+
+    def mm(a, b):
+        return lax.dot_general(a, b, (contract, ((), ())), preferred_element_type=jnp.float32)
+
     return mm(left_high, right_high) + (mm(left_high, right_low) + mm(left_low, right_high))
 
 
-def dot_full(left, right, contract=((1,), (0,))):
+def dot_full(left, right, contract=PLAIN):
     return lax.dot_general(
         left,
         right,
@@ -77,8 +82,8 @@
     )
     starts = jnp.concatenate([jnp.where(inner, block, 0.0) for block in blocks], axis=1)
     nexts = jnp.concatenate([pltpu.roll(block, cols - 1, 1) for block in blocks], axis=1)
-    gram = dot_full(leads, leads, ((1,), (1,)))
-    cross = dot_full(nexts, starts, ((1,), (1,)))
+    gram = dot_full(leads, leads, ACROSS)
+    cross = dot_full(nexts, starts, ACROSS)
     return gram, cross
 
 
@@ -111,7 +116,7 @@
 
 def solve_kernel(core_of, own_ref, other_ref, gram_own_ref, cross_own_ref, vec_ref, val_ref,
                  op_out, res_out, norm_out,
-                 gram_ref, cross_ref, r_ref, x_ref, op_ref, work, res_ref, norm_ref, sems):
+                 gram_ref, cross_ref, r_ref, x_ref, op_ref, work, seen_ref, res_ref, norm_ref, sems):
     width = gram_ref.shape[0]
     core = core_of()
     first = core == 0
@@ -140,8 +145,9 @@
         ends = jnp.where(lane == k, pltpu.roll(series[k], k + 1, 1), ends)
         begin = series[k + 1] if k == 0 else pltpu.roll(series[k + 1], k, 1)
         begins = jnp.where(lane == k, begin, begins)
-    edges = dot_full(begins, ends, ((1,), (1,)))
-    cross_ref[...] = (cross_own_ref[...] + cross_other + edges) * scale
+    edges = dot_full(begins, ends, ACROSS)
+    cross = (cross_own_ref[...] + cross_other + edges) * scale
+    cross_ref[...] = cross
 
     vectors = vec_ref[...]
     eigs = vectors.shape[0]
@@ -154,50 +160,67 @@
     top = jnp.max(jnp.sum(jnp.abs(square), axis=0, keepdims=True), axis=1, keepdims=True)
     bound_squared = top[0, 0]
     top = jnp.maximum(jnp.sqrt(top) * 1.001, 1.5)
-    doublings = jnp.int32(0)
-    for k in range(1, 8):
+    alpha = 2.0 / (top + 1.0)
+    t1 = (top + 1.0) / (top - 1.0)
+    t2 = 2.0 * t1 * t1 - 1.0
+    i2 = 1.0 / t2
+    c = 1.0 + i2
+    r2 = c * (eye - (2.0 * alpha) * gram + (alpha * alpha) * square) - i2 * eye
+    x2 = (c * alpha) * (2.0 * eye - alpha * gram)
+    r_ref[...] = r2
+    x_ref[...] = x2
+
+    def doubled_x(t, x, rp):
+        return (1.0 + 1.0 / t) * (x + dot3(pieces(x), rp))
+
+    def doubled_r(t, rp):
+        return (1.0 + 1.0 / t) * dot3(rp, rp) - (1.0 / t) * eye
+
+    def answer(t, x, cross, gram):
+        xp = pieces(x)
+        guess = dot3(pieces(cross), xp)
+        seen = dot_full(vectors, guess, ACROSS)
+        mixed = dot3(pieces(vectors), xp, ACROSS)
+        rest = pieces(cross - dot_full(guess, gram))
+        last = 1.0 + 1.0 / (2.0 * t * t - 1.0)
+        op_ref[...] = last * (guess + dot3(rest, xp))
+        seen_ref[...] = last * (seen + dot3(pieces(mixed), rest, ACROSS))
+
+    rp2 = pieces(r2)
+    t4 = 2.0 * t2 * t2 - 1.0
+    t8 = 2.0 * t4 * t4 - 1.0
+    x4 = doubled_x(t4, x2, rp2)
+    x8 = doubled_x(t8, x4, pieces(doubled_r(t4, rp2)))
+    answer(t8, x8, cross, gram)
+
+    small, fast = (bound_for(2) / 1.001) ** 2, LARGEST_FAST**2
+    doublings = jnp.int32(1)
+    for k in range(2, 8):
         doublings += (bound_squared > (bound_for(k) / 1.001) ** 2).astype(jnp.int32)
 
-    @pl.when(bound_squared <= LARGEST_FAST**2)
+    @pl.when(jnp.logical_and(bound_squared > small, bound_squared <= fast))
     def _():
-        alpha = 2.0 / (top + 1.0)
-        t1 = (top + 1.0) / (top - 1.0)
-        t2 = 2.0 * t1 * t1 - 1.0
-        i2 = 1.0 / t2
-        c = 1.0 + i2
-        r_ref[...] = c * (eye - (2.0 * alpha) * gram_ref[...] + (alpha * alpha) * square) - i2 * eye
-        x_ref[...] = (c * alpha) * (2.0 * eye - alpha * gram_ref[...])
-
         def double(_, t):
             t = 2.0 * t * t - 1.0
-            it = 1.0 / t
-            x = x_ref[...]
             rp = pieces(r_ref[...])
-            x_ref[...] = (1.0 + it) * (x + dot3(pieces(x), rp))
-            r_ref[...] = (1.0 + it) * dot3(rp, rp) - it * eye
+            x_ref[...] = doubled_x(t, x_ref[...], rp)
+            r_ref[...] = doubled_r(t, rp)
             return t
 
         t = lax.fori_loop(0, doublings, double, t2)
         t = 2.0 * t * t - 1.0
-        x = x_ref[...]
-        x = (1.0 + 1.0 / t) * (x + dot3(pieces(x), pieces(r_ref[...])))
-        x_ref[...] = x
-        xp = pieces(x)
-
-        def refine(guess, xp):
+        x_ref[...] = doubled_x(t, x_ref[...], pieces(r_ref[...]))
+        answer(t, x_ref[...], cross_ref[...], gram_ref[...])
+
+        def again(_, carry):
+            guess = op_ref[...]
             rest = cross_ref[...] - dot_full(guess, gram_ref[...])
-            return guess + dot3(pieces(rest), xp)
-
-        last = 1.0 + 1.0 / (2.0 * t * t - 1.0)
-        op_ref[...] = last * refine(dot3(pieces(cross_ref[...]), xp), xp)
-
-        def again(_, carry):
-            op_ref[...] = refine(op_ref[...], pieces(x_ref[...]))
+            op_ref[...] = guess + dot3(pieces(rest), pieces(x_ref[...]))
             return carry
 
         lax.fori_loop(0, jnp.where(bound_squared > 32.0**2, 3, 0), again, 0)
 
-    @pl.when(bound_squared > LARGEST_FAST**2)
+    @pl.when(bound_squared > fast)
     def _():
         work[:, :width] = gram_ref[...]
         work[:, width:] = cross_ref[...].T
@@ -206,12 +229,18 @@
 
     out = pltpu.make_async_copy(op_ref, op_out, sems.at[0])
     out.start()
-    residual = dot_full(vectors, op_ref[...], ((1,), (1,))) - values * vectors
+
+    @pl.when(bound_squared > 32.0**2)
+    def _():
+        seen_ref[...] = dot_full(vectors, op_ref[...], ACROSS)
+
+    residual = seen_ref[...] - values * vectors
     res_ref[...] = residual
     res = pltpu.make_async_copy(res_ref, res_out, sems.at[1])
     res.start()
-    squares = dot_full(jnp.ones((8, width), jnp.float32), residual * residual, ((1,), (1,)))
-    norm_ref[...] = jnp.sqrt(squares[0] + 1e-06)
+    sums = jnp.sum(residual * residual, axis=1, keepdims=True)
+    sums = jnp.sum(jnp.where(on_diagonal, sums, 0.0), axis=0)
+    norm_ref[...] = jnp.sqrt(sums + 1e-06)
     norm = pltpu.make_async_copy(norm_ref, norm_out, sems.at[2])
     norm.start()
     out.wait()
@@ -236,6 +265,7 @@
         scratch_shapes=[square] * 5
         + [
             pltpu.VMEM((width, 2 * width), jnp.float32),
+            pltpu.VMEM((eigs, width), jnp.float32),
             pltpu.VMEM((eigs, width), jnp.float32),
             pltpu.VMEM((eigs,), jnp.float32),
             pltpu.SemaphoreType.DMA((3,)),

time: 53.6 us -> 57.2 us (1.067); the launches traced: 54.5 us -> 57 us
  Pallas kernels: 16.4 us -> 18.8 us
    pallas_call x1, Pallas kernels: 6.86 us -> 9.34 us  [solve(): pl.pallas_call(functools.partial(solve_kernel, core_of), out_shape=(jax.S...]
where the time goes in v5:
time: 57.2 us; the launch traced here: 57 us
  blocking collectives  33.4 us (58%)
  Pallas kernels  18.8 us (33%)
  starting transfers between devices  3.44 us (6%)
  between operations  0.67 us (1%)
    all_to_all x1, blocking collectives, body(): lax.all_to_all(partial_value.reshape(rows, lines, block_cols), 'rows', 0,...  19.9 us
    all_to_all x1, blocking collectives, body(): lax.all_to_all(jnp.broadcast_to(own_lines[None], (2 * rows, lines, block_...  13.5 us
    pallas_call x1, Pallas kernels, solve(): pl.pallas_call(functools.partial(solve_kernel, core_of), out_shape=(jax.S...  9.34 us
    pallas_call x1, Pallas kernels, project(): pl.pallas_call(functools.partial(project_kernel, chunk), out_shape=jax.Sh...  8.87 us
    ppermute x1, starting transfers between devices, body(): other = lax.ppermute(gathered, axes, swap)  3.44 us
  transfers between devices with their start and end apart: 1, of which 1 were waited for; matrix products, arithmetic and copies ran while one was open for 0% of the time, Pallas kernels for 1%

profile of v5, /device:TPU:1, one launch (start us, length us, event | category | flops | bytes accessed | tf_op | source)
XLA Modules:
  0.0 57.0 jit_solution(13495745752568389729)
XLA Ops:
  0.6 0.0 copy-start.1
  0.6 0.0 copy-start
  0.7 8.9 %project.1 = f32[256,128]{1,0:T(8,128)S(1)} custom-call(bf16[32768,256]{1,0:T(8,128)(2,1)} %modes_hbm.1, bf16[32768,128]{1,0:T(8,128)(2,1)} %snaps_hbm.1), custom_call_target="tpu_custom_call" | custom-call | tf_op jit(solution)/shard_map/project/pallas_call | solution.py:313
  9.5 19.9 %all_to_all.10 = f32[32,8,128]{2,1,0:T(8,128)S(1)} all-to-all(f32[32,8,128]{2,1,0:T(8,128)S(1)} %bitcast.5), channel_id=1, replica_groups=mesh['rows'=32,'tm'=4] {'rows'}, dimensions={0} | all-to-all | bytes 262144 | tf_op jit(solution)/shard_map/all_to_all | solution.py:341
  29.5 13.5 %all_to_all.11 = f32[64,8,128]{2,1,0:T(8,128)S(1)} all-to-all(f32[64,8,128]{2,1,0:T(8,128)S(1)} %broadcast_in_dim.2), channel_id=1, replica_groups={{0,2,4,6,8,10,12,14,16,18,20,22,24,26,28,30,32,34,36,38,40,42,44,46,48,..., dimensions={0} | all-to-all | bytes 524288 | tf_op jit(solution)/shard_map/all_to_all | solution.py:346
  43.0 3.4 %collective-permute-start = (f32[64,8,128]{2,1,0:T(8,128)S(1)}, f32[64,8,128]{2,1,0:T(8,128)S(1)}, u32[]{:S(2)}, u32[]{:S(2)}) collective-permute-start(f32[64,8,128]{2,1,0:T(8,128)S(1)} %all_to_all.11), channel_id=1, source_target_pairs={{0,1},{1,0},{2,3},{3,2},{4,5},{5,4},{6,7},{7,6},{8,9},{9,8},{10,11... | collective-permute-start | bytes 786440 | tf_op jit(solution)/shard_map/ppermute | solution.py:355
  46.5 0.6 %own_sums.1 = (f32[256,256]{1,0:T(8,128)S(1)}, f32[256,256]{1,0:T(8,128)S(1)}) custom-call(f32[32,2,8,128]{3,2,1,0:T(8,128)S(1)} %bitcast.3), custom_call_target="tpu_custom_call" | custom-call | flops 402653184 | bytes 786432 | tf_op jit(solution)/shard_map/own_sums/pallas_call | solution.py:104
  47.1 0.5 collective-permute-done
  47.6 0.0 copy-done.1
  47.6 0.0 copy-done
  47.6 9.3 %solve.1 = (f32[256,256]{1,0:T(8,128)}, f32[3,256]{1,0:T(4,128)}, f32[3]{0:T(128)}) custom-call(f32[32,2,8,128]{3,2,1,0:T(8,128)S(1)} %bitcast.4, f32[32,2,8,128]{3,2,1,0:T(8,128)S(1)} %bitcast.6, f32[256,256]{1,0:T(8,128)S(1)} %get-tuple-element.5.gram_own_ref, f32[256,256]{1,0:T(8,128)S(1)} %get-tuple-element.6.cross_own_ref, f32[3,256]{1,0:T(4,128)S(1)} %copy-done, ...), custom_call_target="tpu_custom_call" | custom-call | tf_op jit(solution)/shard_map/solve/pallas_call | solution.py:256
  (2 shorter events, 0.1 us)
Async XLA Ops:
  0.6 47.0 %copy-start.1 = (f32[3]{0:T(128)S(1)}, f32[3]{0:T(128)}, u32[]{:S(2)}) copy-start(f32[3]{0:T(128)} %val_ref.1) | copy-start | bytes 40
  0.6 47.0 %copy-start = (f32[3,256]{1,0:T(4,128)S(1)}, f32[3,256]{1,0:T(4,128)}, u32[]{:S(2)}) copy-start(f32[3,256]{1,0:T(4,128)} %vec_ref.1) | copy-start | bytes 9220
  43.0 4.6 %collective-permute-start = (f32[64,8,128]{2,1,0:T(8,128)S(1)}, f32[64,8,128]{2,1,0:T(8,128)S(1)}, u32[]{:S(2)}, u32[]{:S(2)}) collective-permute-start(f32[64,8,128]{2,1,0:T(8,128)S(1)} %all_to_all.11), channel_id=1, source_target_pairs={{0,1},{1,0},{2,3},{3,2},{4,5},{5,4},{6,7},{7,6},{8,9},{9,8},{10,11... | collective-permute-start | bytes 786440 | tf_op jit(solution)/shard_map/ppermute | solution.py:355

commit v6 on v4

--- a/solution.py
+++ b/solution.py
@@ -10,6 +10,7 @@
 
 LARGEST_FAST = 2048.0
 RESIDUAL_FLOOR = 224.0
+PLANES = 2
 PLAIN = ((1,), (0,))
 ACROSS = ((1,), (1,))
 
@@ -264,50 +265,44 @@
 
 def project_kernel(chunk, modes_hbm, snaps_hbm, out, modes_vmem, snaps_vmem, total, mode_sem, snap_sem):
     steps = modes_hbm.shape[0] // chunk
-    tail = chunk // 2
-
-    def copies(step, start, size):
-        lines = pl.ds(start, size)
+
+    def copies(step):
+        lines = pl.ds(step * chunk, chunk)
         return (
             pltpu.make_async_copy(modes_hbm.at[lines], modes_vmem.at[lines], mode_sem.at[step]),
             pltpu.make_async_copy(snaps_hbm.at[lines], snaps_vmem.at[lines], snap_sem.at[step]),
         )
 
-    pieces_of = [(step, step * chunk, chunk) for step in range(steps - 1)]
-    pieces_of += [(steps - 1 + k, (steps - 1) * chunk + k * tail, tail) for k in range(2)]
-    for piece in pieces_of:
-        for copy in copies(*piece):
+    for step in range(steps):
+        for copy in copies(step):
             copy.start()
-
-    def product(step, start, size):
-        for copy in copies(step, start, size):
+    total[...] = jnp.zeros_like(total)
+
+    def add(step, carry):
+        for copy in copies(step):
             copy.wait()
-        lines = pl.ds(start, size)
-        return lax.dot_general(
+        lines = pl.ds(pl.multiple_of(step * chunk, chunk), chunk)
+        total[...] += lax.dot_general(
             snaps_vmem[lines, :],
             modes_vmem[lines, :],
             (((0,), (0,)), ((), ())),
             preferred_element_type=jnp.float32,
         )
-
-    total[...] = product(0, 0, chunk)
-
-    def add(step, carry):
-        total[...] += product(step, pl.multiple_of(step * chunk, chunk), chunk)
         return carry
 
-    lax.fori_loop(1, steps - 1, add, 0)
-    total[...] += product(*pieces_of[-2])
-    out[...] = (total[...] + product(*pieces_of[-1])).T
+    lax.fori_loop(0, steps, add, 0)
+    sums = total[...].T
+    for copy in range(PLANES):
+        out[copy] = sums
 
 
 def project(modes, snapshots, chunk=2048):
     width, cols = modes.shape[1], snapshots.shape[1]
-    steps = modes.shape[0] // chunk + 1
+    steps = modes.shape[0] // chunk
     far = functools.partial(pltpu.with_memory_space_constraint, memory_space=pltpu.HBM)
     return pl.pallas_call(
         functools.partial(project_kernel, chunk),
-        out_shape=jax.ShapeDtypeStruct((width, cols), jnp.float32),
+        out_shape=jax.ShapeDtypeStruct((PLANES, width, cols), jnp.float32),
         in_specs=[pl.BlockSpec(memory_space=pltpu.HBM)] * 2,
         out_specs=pl.BlockSpec(memory_space=pltpu.VMEM),
         scratch_shapes=[
@@ -322,33 +317,37 @@
     )(far(modes), far(snapshots))
 
 
-def joint_groups():
-    rows, halves = 32, 2
-    return [[r * 4 + 2 * half + core for r in range(rows) for half in range(halves)] for core in range(2)]
+def gather_groups(rows, times):
+    plane = rows // PLANES
+    return [
+        [(high * plane + r) * times + 2 * low + core for r in range(plane) for low in range(2)]
+        for high in range(PLANES)
+        for core in range(2)
+    ]
 
 
 def body(snapshots, modes, eig_vectors, eig_values):
     width = modes.shape[1]
     block_cols = snapshots.shape[1]
-    rows = lax.axis_size("rows")
+    rows, times = lax.axis_size("rows"), lax.axis_size("tm")
+    plane = rows // PLANES
+    lines = width // plane
     partial_value = project(modes, snapshots)
-    lines = width // rows
     arrived = lax.all_to_all(
         partial_value.reshape(rows, lines, block_cols), "rows", 0, 0, tiled=True
     )
     own_lines = jnp.sum(arrived, axis=0)
     axes = ("rows", "tm")
     gathered = lax.all_to_all(
-        jnp.broadcast_to(own_lines[None], (2 * rows, lines, block_cols)),
+        jnp.broadcast_to(own_lines[None], (2 * plane, lines, block_cols)),
         axes,
         0,
         0,
         tiled=True,
-        axis_index_groups=joint_groups(),
-    )
-    swap = [(i, i ^ 1) for i in range(4 * rows)]
-    other = lax.ppermute(gathered, axes, swap)
-    shape = (rows, 2, lines, block_cols)
+        axis_index_groups=gather_groups(rows, times),
+    )
+    other = lax.ppermute(gathered, axes, [(i, i ^ 1) for i in range(times * rows)])
+    shape = (plane, 2, lines, block_cols)
     own, other = gathered.reshape(shape), other.reshape(shape)
     gram_own, cross_own = own_sums(own, width)
     return solve(own, other, gram_own, cross_own, eig_vectors, eig_values)

time: 55.1 us -> 53.9 us (0.978)
  blocking collectives: 33.4 us -> 32.5 us
    all_to_all x1, blocking collectives: 13.5 us -> 12 us  [body(): lax.all_to_all(jnp.broadcast_to(own_lines[None], (2 * plane, lines, block...]
where the time goes in v6:
time: 53.9 us; the launch traced here: 53.7 us
  blocking collectives  32.5 us (60%)
  Pallas kernels  16.5 us (31%)
  starting transfers between devices  3.45 us (6%)
  between operations  0.68 us (1%)
    all_to_all x1, blocking collectives, body(): lax.all_to_all(partial_value.reshape(rows, lines, block_cols), 'rows', 0,...  20.4 us
    all_to_all x1, blocking collectives, body(): lax.all_to_all(jnp.broadcast_to(own_lines[None], (2 * plane, lines, block...  12 us
    pallas_call x1, Pallas kernels, project(): pl.pallas_call(functools.partial(project_kernel, chunk), out_shape=jax.Sh...  8.87 us
    pallas_call x1, Pallas kernels, solve(): pl.pallas_call(functools.partial(solve_kernel, core_of), out_shape=(jax.S...  7.01 us
    ppermute x1, starting transfers between devices, body(): lax.ppermute(gathered, axes, [(i, i ^ 1) for i in range(times * rows)])  3.45 us
  transfers between devices with their start and end apart: 1, of which 1 were waited for; matrix products, arithmetic and copies ran while one was open for 0% of the time, Pallas kernels for 1%

profile of v6, /device:TPU:1, one launch (start us, length us, event | category | flops | bytes accessed | tf_op | source)
XLA Modules:
  0.0 53.7 jit_solution(9409486874842334120)
XLA Ops:
  0.6 0.0 copy-start.1
  0.6 0.0 copy-start
  0.7 8.9 %project.1 = f32[2,256,128]{2,1,0:T(8,128)S(1)} custom-call(bf16[32768,256]{1,0:T(8,128)(2,1)} %modes_hbm.1, bf16[32768,128]{1,0:T(8,128)(2,1)} %snaps_hbm.1), custom_call_target="tpu_custom_call" | custom-call | tf_op jit(solution)/shard_map/project/pallas_call | solution.py:303
  9.5 20.4 %all_to_all.10 = f32[32,16,128]{2,1,0:T(8,128)S(1)} all-to-all(f32[32,16,128]{2,1,0:T(8,128)S(1)} %bitcast.3), channel_id=1, replica_groups=mesh['rows'=32,'tm'=4] {'rows'}, dimensions={0} | all-to-all | bytes 524288 | tf_op jit(solution)/shard_map/all_to_all | solution.py:336
  30.0 12.0 %all_to_all.11 = f32[32,16,128]{2,1,0:T(8,128)S(1)} all-to-all(f32[32,16,128]{2,1,0:T(8,128)S(1)} %broadcast_in_dim.2), channel_id=1, replica_groups={{0,2,4,6,8,10,12,14,16,18,20,22,24,26,28,30,32,34,36,38,40,42,44,46,48,..., dimensions={0} | all-to-all | bytes 524288 | tf_op jit(solution)/shard_map/all_to_all | solution.py:341
  42.1 3.5 %collective-permute-start = (f32[32,16,128]{2,1,0:T(8,128)S(1)}, f32[32,16,128]{2,1,0:T(8,128)S(1)}, u32[]{:S(2)}, u32[]{:S(2)}) collective-permute-start(f32[32,16,128]{2,1,0:T(8,128)S(1)} %all_to_all.11), channel_id=1, source_target_pairs={{0,1},{1,0},{2,3},{3,2},{4,5},{5,4},{6,7},{7,6},{8,9},{9,8},{10,11... | collective-permute-start | bytes 786440 | tf_op jit(solution)/shard_map/ppermute | solution.py:349
  45.5 0.6 %own_sums.1 = (f32[256,256]{1,0:T(8,128)S(1)}, f32[256,256]{1,0:T(8,128)S(1)}) custom-call(f32[16,2,16,128]{3,2,1,0:T(8,128)S(1)} %bitcast.4), custom_call_target="tpu_custom_call" | custom-call | flops 402653184 | bytes 786432 | tf_op jit(solution)/shard_map/own_sums/pallas_call | solution.py:105
  46.2 0.5 collective-permute-done
  46.7 0.0 copy-done.1
  46.7 0.0 copy-done
  46.7 7.0 %solve.1 = (f32[256,256]{1,0:T(8,128)}, f32[3,256]{1,0:T(4,128)}, f32[3]{0:T(128)}) custom-call(f32[16,2,16,128]{3,2,1,0:T(8,128)S(1)} %bitcast.5, f32[16,2,16,128]{3,2,1,0:T(8,128)S(1)} %bitcast.6, f32[256,256]{1,0:T(8,128)S(1)} %get-tuple-element.5.gram_own_ref, f32[256,256]{1,0:T(8,128)S(1)} %get-tuple-element.6.cross_own_ref, f32[3,256]{1,0:T(4,128)S(1)} %copy-done, ...), custom_call_target="tpu_custom_call" | custom-call | tf_op jit(solution)/shard_map/solve/pallas_call | solution.py:244
  (2 shorter events, 0.1 us)
Async XLA Ops:
  0.6 46.1 %copy-start.1 = (f32[3]{0:T(128)S(1)}, f32[3]{0:T(128)}, u32[]{:S(2)}) copy-start(f32[3]{0:T(128)} %val_ref.1) | copy-start | bytes 40
  0.6 46.1 %copy-start = (f32[3,256]{1,0:T(4,128)S(1)}, f32[3,256]{1,0:T(4,128)}, u32[]{:S(2)}) copy-start(f32[3,256]{1,0:T(4,128)} %vec_ref.1) | copy-start | bytes 9220
  42.1 4.6 %collective-permute-start = (f32[32,16,128]{2,1,0:T(8,128)S(1)}, f32[32,16,128]{2,1,0:T(8,128)S(1)}, u32[]{:S(2)}, u32[]{:S(2)}) collective-permute-start(f32[32,16,128]{2,1,0:T(8,128)S(1)} %all_to_all.11), channel_id=1, source_target_pairs={{0,1},{1,0},{2,3},{3,2},{4,5},{5,4},{6,7},{7,6},{8,9},{9,8},{10,11... | collective-permute-start | bytes 786440 | tf_op jit(solution)/shard_map/ppermute | solution.py:349

commit v7 on v6

--- a/solution.py
+++ b/solution.py
@@ -10,7 +10,6 @@
 
 LARGEST_FAST = 2048.0
 RESIDUAL_FLOOR = 224.0
-PLANES = 2
 PLAIN = ((1,), (0,))
 ACROSS = ((1,), (1,))
 
@@ -263,7 +262,7 @@
     )(*map(near, (own, other, gram_own, cross_own, vectors, values)))
 
 
-def project_kernel(chunk, modes_hbm, snaps_hbm, out, modes_vmem, snaps_vmem, total, mode_sem, snap_sem):
+def project_kernel(chunk, owner, lines, modes_hbm, snaps_hbm, out, modes_vmem, snaps_vmem, total, mode_sem, snap_sem):
     steps = modes_hbm.shape[0] // chunk
 
     def copies(step):
@@ -292,17 +291,17 @@
 
     lax.fori_loop(0, steps, add, 0)
     sums = total[...].T
-    for copy in range(PLANES):
-        out[copy] = sums
-
-
-def project(modes, snapshots, chunk=2048):
+    for place, block in enumerate(owner):
+        out[place] = sums[block * lines : (block + 1) * lines]
+
+
+def project(modes, snapshots, owner, lines, chunk=2048):
     width, cols = modes.shape[1], snapshots.shape[1]
     steps = modes.shape[0] // chunk
     far = functools.partial(pltpu.with_memory_space_constraint, memory_space=pltpu.HBM)
     return pl.pallas_call(
-        functools.partial(project_kernel, chunk),
-        out_shape=jax.ShapeDtypeStruct((PLANES, width, cols), jnp.float32),
+        functools.partial(project_kernel, chunk, owner, lines),
+        out_shape=jax.ShapeDtypeStruct((len(owner), lines, cols), jnp.float32),
         in_specs=[pl.BlockSpec(memory_space=pltpu.HBM)] * 2,
         out_specs=pl.BlockSpec(memory_space=pltpu.VMEM),
         scratch_shapes=[
@@ -317,37 +316,55 @@
     )(far(modes), far(snapshots))
 
 
-def gather_groups(rows, times):
-    plane = rows // PLANES
-    return [
-        [(high * plane + r) * times + 2 * low + core for r in range(plane) for low in range(2)]
-        for high in range(PLANES)
+DIMS = "YZzXx"
+FIRST = 'ZzXx'
+COPIES = 'X'
+
+
+def plan(rows, times):
+    kept = [d for d in DIMS if d in FIRST and d not in COPIES]
+    partial = [d for d in DIMS if d not in FIRST]
+    places = [dict(zip(DIMS, ((r >> (4 - k)) & 1 for k in range(5)))) for r in range(rows)]
+
+    def packed(place, dims):
+        return sum(place[d] << k for k, d in enumerate(reversed(dims)))
+
+    owner = [packed(place, kept) for place in places]
+    first, second = {}, {}
+    for r, place in enumerate(places):
+        first.setdefault(packed(place, partial), []).append(r)
+        second.setdefault(packed(place, list(COPIES)), []).append((packed(place, partial + kept), r))
+    members = [first[k] for k in sorted(first)]
+    gathers = [
+        [r * times + 2 * low + core for _, r in sorted(second[k]) for low in range(2)]
+        for k in sorted(second)
         for core in range(2)
     ]
+    return [owner[r] for r in members[0]], members, gathers, 2 ** len(kept), 2 ** len(partial)
 
 
 def body(snapshots, modes, eig_vectors, eig_values):
     width = modes.shape[1]
     block_cols = snapshots.shape[1]
     rows, times = lax.axis_size("rows"), lax.axis_size("tm")
-    plane = rows // PLANES
-    lines = width // plane
-    partial_value = project(modes, snapshots)
-    arrived = lax.all_to_all(
-        partial_value.reshape(rows, lines, block_cols), "rows", 0, 0, tiled=True
-    )
+    owner, members, gathers, owners, parts = plan(rows, times)
+    lines = width // owners
+    sent = project(modes, snapshots, owner, lines)
+    arrived = lax.all_to_all(sent, "rows", 0, 0, tiled=True, axis_index_groups=members)
     own_lines = jnp.sum(arrived, axis=0)
     axes = ("rows", "tm")
     gathered = lax.all_to_all(
-        jnp.broadcast_to(own_lines[None], (2 * plane, lines, block_cols)),
+        jnp.broadcast_to(own_lines[None], (2 * owners * parts, lines, block_cols)),
         axes,
         0,
         0,
         tiled=True,
-        axis_index_groups=gather_groups(rows, times),
-    )
+        axis_index_groups=gathers,
+    )
+    if parts > 1:
+        gathered = jnp.sum(gathered.reshape(parts, 2 * owners, lines, block_cols), axis=0)
     other = lax.ppermute(gathered, axes, [(i, i ^ 1) for i in range(times * rows)])
-    shape = (plane, 2, lines, block_cols)
+    shape = (owners, 2, lines, block_cols)
     own, other = gathered.reshape(shape), other.reshape(shape)
     gram_own, cross_own = own_sums(own, width)
     return solve(own, other, gram_own, cross_own, eig_vectors, eig_values)

time: 53.9 us -> 51.5 us (0.955)
  blocking collectives: 32.5 us -> 29.9 us
    all_to_all x2, blocking collectives: 32.5 us -> 29.9 us  [the longest x1 15.8 us: body(): lax.all_to_all(sent, 'rows', 0, 0, tiled=True, axis_index_groups=members)]
where the time goes in v7:
time: 51.5 us; the launch traced here: 51.3 us
  blocking collectives  29.9 us (58%)
  Pallas kernels  16.5 us (32%)
  starting transfers between devices  3.52 us (7%)
  between operations  0.68 us (1%)
  waiting for transfers between devices  0.52 us (1%)
    all_to_all x1, blocking collectives, body(): lax.all_to_all(sent, 'rows', 0, 0, tiled=True, axis_index_groups=members)  15.8 us
    all_to_all x1, blocking collectives, body(): lax.all_to_all(jnp.broadcast_to(own_lines[None], (2 * owners * parts, lin...  14.2 us
    pallas_call x1, Pallas kernels, project(): pl.pallas_call(functools.partial(project_kernel, chunk, owner, lines), ou...  8.87 us
    pallas_call x1, Pallas kernels, solve(): pl.pallas_call(functools.partial(solve_kernel, core_of), out_shape=(jax.S...  7.01 us
    ppermute x1, starting transfers between devices, body(): lax.ppermute(gathered, axes, [(i, i ^ 1) for i in range(times * rows)])  3.52 us
  transfers between devices with their start and end apart: 1, of which 1 were waited for; matrix products, arithmetic and copies ran while one was open for 0% of the time, Pallas kernels for 1%

profile of v7, /device:TPU:1, one launch (start us, length us, event | category | flops | bytes accessed | tf_op | source)
XLA Modules:
  0.0 51.3 jit_solution(3986648072747511262)
XLA Ops:
  0.6 0.0 copy-start.1
  0.6 0.0 copy-start
  0.7 8.9 %project.1 = f32[16,32,128]{2,1,0:T(8,128)S(1)} custom-call(bf16[32768,256]{1,0:T(8,128)(2,1)} %modes_hbm.1, bf16[32768,128]{1,0:T(8,128)(2,1)} %snaps_hbm.1), custom_call_target="tpu_custom_call" | custom-call | tf_op jit(solution)/shard_map/project/pallas_call | solution.py:302
  9.5 15.8 %all_to_all.10 = f32[16,32,128]{2,1,0:T(8,128)S(1)} all-to-all(f32[16,32,128]{2,1,0:T(8,128)S(1)} %project.1), channel_id=1, replica_groups={{0,4,8,12,16,20,24,28,32,36,40,44,48,52,56,60},{64,68,72,76,80,84,88,92..., dimensions={0} | all-to-all | bytes 524288 | tf_op jit(solution)/shard_map/all_to_all | solution.py:353
  25.3 0.1 broadcast_in_dim.2
  25.4 14.2 %all_to_all.11 = f32[32,32,128]{2,1,0:T(8,128)S(1)} all-to-all(f32[32,32,128]{2,1,0:T(8,128)S(1)} %broadcast_in_dim.2), channel_id=1, replica_groups={{0,2,4,6,16,18,20,22,32,34,36,38,48,50,52,54,64,66,68,70,80,82,84,86,96..., dimensions={0} | all-to-all | bytes 1048576 | tf_op jit(solution)/shard_map/all_to_all | solution.py:356
  39.6 3.5 %collective-permute-start = (f32[16,32,128]{2,1,0:T(8,128)S(1)}, f32[16,32,128]{2,1,0:T(8,128)S(1)}, u32[]{:S(2)}, u32[]{:S(2)}) collective-permute-start(f32[16,32,128]{2,1,0:T(8,128)S(1)} %reduce_sum.19), channel_id=1, source_target_pairs={{0,1},{1,0},{2,3},{3,2},{4,5},{5,4},{6,7},{7,6},{8,9},{9,8},{10,11... | collective-permute-start | bytes 786440 | tf_op jit(solution)/shard_map/ppermute | solution.py:366
  43.1 0.6 %own_sums.1 = (f32[256,256]{1,0:T(8,128)S(1)}, f32[256,256]{1,0:T(8,128)S(1)}) custom-call(f32[8,2,32,128]{3,2,1,0:T(8,128)S(1)} %bitcast.3), custom_call_target="tpu_custom_call" | custom-call | flops 402653184 | bytes 786432 | tf_op jit(solution)/shard_map/own_sums/pallas_call | solution.py:104
  43.7 0.5 %collective-permute-done = f32[16,32,128]{2,1,0:T(8,128)S(1)} collective-permute-done((f32[16,32,128]{2,1,0:T(8,128)S(1)}, f32[16,32,128]{2,1,0:T(8,128)S(1)}, u32[]{:S(2)}, u32[]{:S(2)}) %collective-permute-start) | collective-permute-done | bytes 262176 | tf_op jit(solution)/shard_map/ppermute | solution.py:366
  44.3 0.0 copy-done.1
  44.3 0.0 copy-done
  44.3 7.0 %solve.1 = (f32[256,256]{1,0:T(8,128)}, f32[3,256]{1,0:T(4,128)}, f32[3]{0:T(128)}) custom-call(f32[8,2,32,128]{3,2,1,0:T(8,128)S(1)} %bitcast.4, f32[8,2,32,128]{3,2,1,0:T(8,128)S(1)} %bitcast.5, f32[256,256]{1,0:T(8,128)S(1)} %get-tuple-element.5.gram_own_ref, f32[256,256]{1,0:T(8,128)S(1)} %get-tuple-element.6.cross_own_ref, f32[3,256]{1,0:T(4,128)S(1)} %copy-done, ...), custom_call_target="tpu_custom_call" | custom-call | tf_op jit(solution)/shard_map/solve/pallas_call | solution.py:243
  (2 shorter events, 0.1 us)
Async XLA Ops:
  0.6 43.6 %copy-start.1 = (f32[3]{0:T(128)S(1)}, f32[3]{0:T(128)}, u32[]{:S(2)}) copy-start(f32[3]{0:T(128)} %val_ref.1) | copy-start | bytes 40
  0.6 43.6 %copy-start = (f32[3,256]{1,0:T(4,128)S(1)}, f32[3,256]{1,0:T(4,128)}, u32[]{:S(2)}) copy-start(f32[3,256]{1,0:T(4,128)} %vec_ref.1) | copy-start | bytes 9220
  39.6 4.7 %collective-permute-start = (f32[16,32,128]{2,1,0:T(8,128)S(1)}, f32[16,32,128]{2,1,0:T(8,128)S(1)}, u32[]{:S(2)}, u32[]{:S(2)}) collective-permute-start(f32[16,32,128]{2,1,0:T(8,128)S(1)} %reduce_sum.19), channel_id=1, source_target_pairs={{0,1},{1,0},{2,3},{3,2},{4,5},{5,4},{6,7},{7,6},{8,9},{9,8},{10,11... | collective-permute-start | bytes 786440 | tf_op jit(solution)/shard_map/ppermute | solution.py:366

commit v8 on v7

--- a/solution.py
+++ b/solution.py
@@ -333,8 +333,8 @@
     first, second = {}, {}
     for r, place in enumerate(places):
         first.setdefault(packed(place, partial), []).append(r)
-        second.setdefault(packed(place, list(COPIES)), []).append((packed(place, partial + kept), r))
-    members = [first[k] for k in sorted(first)]
+        second.setdefault(packed(place, list(COPIES)), []).append((packed(place, kept + partial), r))
+    members = [sorted(first[k], key=lambda r: packed(places[r], 'zxZX')) for k in sorted(first)]
     gathers = [
         [r * times + 2 * low + core for _, r in sorted(second[k]) for low in range(2)]
         for k in sorted(second)
@@ -362,7 +362,7 @@
         axis_index_groups=gathers,
     )
     if parts > 1:
-        gathered = jnp.sum(gathered.reshape(parts, 2 * owners, lines, block_cols), axis=0)
+        gathered = jnp.sum(gathered.reshape(owners, parts, 2, lines, block_cols), axis=1)
     other = lax.ppermute(gathered, axes, [(i, i ^ 1) for i in range(times * rows)])
     shape = (owners, 2, lines, block_cols)
     own, other = gathered.reshape(shape), other.reshape(shape)

time: 51.5 us -> 51.1 us (level)
  no operation moved by 1% of the time
where the time goes in v8:
time: 51.1 us; the launch traced here: 50.9 us
  blocking collectives  30.1 us (59%)
  Pallas kernels  16.5 us (32%)
  starting transfers between devices  3.04 us (6%)
  between operations  0.68 us (1%)
  waiting for transfers between devices  0.52 us (1%)
    all_to_all x1, blocking collectives, body(): lax.all_to_all(sent, 'rows', 0, 0, tiled=True, axis_index_groups=members)  16 us
    all_to_all x1, blocking collectives, body(): lax.all_to_all(jnp.broadcast_to(own_lines[None], (2 * owners * parts, lin...  14.1 us
    pallas_call x1, Pallas kernels, project(): pl.pallas_call(functools.partial(project_kernel, chunk, owner, lines), ou...  8.87 us
    pallas_call x1, Pallas kernels, solve(): pl.pallas_call(functools.partial(solve_kernel, core_of), out_shape=(jax.S...  6.99 us
    ppermute x1, starting transfers between devices, body(): lax.ppermute(gathered, axes, [(i, i ^ 1) for i in range(times * rows)])  3.04 us
  transfers between devices with their start and end apart: 1, of which 1 were waited for; matrix products, arithmetic and copies ran while one was open for 0% of the time, Pallas kernels for 1%

profile of v8, /device:TPU:1, one launch (start us, length us, event | category | flops | bytes accessed | tf_op | source)
XLA Modules:
  0.0 50.9 jit_solution(6012381708376447842)
XLA Ops:
  0.6 0.0 copy-start.1
  0.6 0.0 copy-start
  0.7 8.9 %project.1 = f32[16,32,128]{2,1,0:T(8,128)S(1)} custom-call(bf16[32768,256]{1,0:T(8,128)(2,1)} %modes_hbm.1, bf16[32768,128]{1,0:T(8,128)(2,1)} %snaps_hbm.1), custom_call_target="tpu_custom_call" | custom-call | tf_op jit(solution)/shard_map/project/pallas_call | solution.py:302
  9.5 16.0 %all_to_all.10 = f32[16,32,128]{2,1,0:T(8,128)S(1)} all-to-all(f32[16,32,128]{2,1,0:T(8,128)S(1)} %project.1), channel_id=1, replica_groups={{0,8,32,40,4,12,36,44,16,24,48,56,20,28,52,60},{64,72,96,104,68,76,100,..., dimensions={0} | all-to-all | bytes 524288 | tf_op jit(solution)/shard_map/all_to_all | solution.py:353
  25.5 0.1 broadcast_in_dim.2
  25.6 14.1 %all_to_all.11 = f32[32,32,128]{2,1,0:T(8,128)S(1)} all-to-all(f32[32,32,128]{2,1,0:T(8,128)S(1)} %broadcast_in_dim.2), channel_id=1, replica_groups={{0,2,64,66,4,6,68,70,16,18,80,82,20,22,84,86,32,34,96,98,36,38,100,102,..., dimensions={0} | all-to-all | bytes 1048576 | tf_op jit(solution)/shard_map/all_to_all | solution.py:356
  39.7 3.0 %collective-permute-start = (f32[8,2,32,128]{3,2,1,0:T(8,128)S(1)}, f32[8,2,32,128]{3,2,1,0:T(8,128)S(1)}, u32[]{:S(2)}, u32[]{:S(2)}) collective-permute-start(f32[8,2,32,128]{3,2,1,0:T(8,128)S(1)} %reduce_sum.19.own_ref), channel_id=1, source_target_pairs={{0,1},{1,0},{2,3},{3,2},{4,5},{5,4},{6,7},{7,6},{8,9},{9,8},{10,11... | collective-permute-start | bytes 786440 | tf_op jit(solution)/shard_map/ppermute | solution.py:366
  42.8 0.6 %own_sums.1 = (f32[256,256]{1,0:T(8,128)S(1)}, f32[256,256]{1,0:T(8,128)S(1)}) custom-call(f32[8,2,32,128]{3,2,1,0:T(8,128)S(1)} %reduce_sum.19.own_ref), custom_call_target="tpu_custom_call" | custom-call | flops 402653184 | bytes 786432 | tf_op jit(solution)/shard_map/own_sums/pallas_call | solution.py:104
  43.4 0.5 %collective-permute-done.other_ref = f32[8,2,32,128]{3,2,1,0:T(8,128)S(1)} collective-permute-done((f32[8,2,32,128]{3,2,1,0:T(8,128)S(1)}, f32[8,2,32,128]{3,2,1,0:T(8,128)S(1)}, u32[]{:S(2)}, u32[]{:S(2)}) %collective-permute-start) | collective-permute-done | bytes 262176 | tf_op jit(solution)/shard_map/ppermute | solution.py:366
  43.9 0.0 copy-done.1
  43.9 0.0 copy-done
  43.9 7.0 %solve.1 = (f32[256,256]{1,0:T(8,128)}, f32[3,256]{1,0:T(4,128)}, f32[3]{0:T(128)}) custom-call(f32[8,2,32,128]{3,2,1,0:T(8,128)S(1)} %reduce_sum.19.own_ref, f32[8,2,32,128]{3,2,1,0:T(8,128)S(1)} %collective-permute-done.other_ref, f32[256,256]{1,0:T(8,128)S(1)} %get-tuple-element.5.gram_own_ref, f32[256,256]{1,0:T(8,128)S(1)} %get-tuple-element.6.cross_own_ref, ...), custom_call_target="tpu_custom_call" | custom-call | tf_op jit(solution)/shard_map/solve/pallas_call | solution.py:243
  (2 shorter events, 0.1 us)
Async XLA Ops:
  0.6 43.3 %copy-start.1 = (f32[3]{0:T(128)S(1)}, f32[3]{0:T(128)}, u32[]{:S(2)}) copy-start(f32[3]{0:T(128)} %val_ref.1) | copy-start | bytes 40
  0.6 43.3 %copy-start = (f32[3,256]{1,0:T(4,128)S(1)}, f32[3,256]{1,0:T(4,128)}, u32[]{:S(2)}) copy-start(f32[3,256]{1,0:T(4,128)} %vec_ref.1) | copy-start | bytes 9220
  39.7 4.2 %collective-permute-start = (f32[8,2,32,128]{3,2,1,0:T(8,128)S(1)}, f32[8,2,32,128]{3,2,1,0:T(8,128)S(1)}, u32[]{:S(2)}, u32[]{:S(2)}) collective-permute-start(f32[8,2,32,128]{3,2,1,0:T(8,128)S(1)} %reduce_sum.19.own_ref), channel_id=1, source_target_pairs={{0,1},{1,0},{2,3},{3,2},{4,5},{5,4},{6,7},{7,6},{8,9},{9,8},{10,11... | collective-permute-start | bytes 786440 | tf_op jit(solution)/shard_map/ppermute | solution.py:366

commit v9 on v8

--- a/solution.py
+++ b/solution.py
@@ -9,7 +9,7 @@
 from jax.sharding import PartitionSpec as P
 
 LARGEST_FAST = 2048.0
-RESIDUAL_FLOOR = 224.0
+RESIDUAL_FLOOR = 150.0
 PLAIN = ((1,), (0,))
 ACROSS = ((1,), (1,))
 
@@ -160,7 +160,7 @@
     bound_squared = top[0, 0]
     top = jnp.maximum(jnp.sqrt(top) * 1.001, 1.5)
     doublings = jnp.int32(0)
-    for k in range(1, 8):
+    for k in range(2, 8):
         doublings += (bound_squared > (bound_for(k) / 1.001) ** 2).astype(jnp.int32)
 
     @pl.when(bound_squared <= LARGEST_FAST**2)
@@ -170,22 +170,30 @@
         t2 = 2.0 * t1 * t1 - 1.0
         i2 = 1.0 / t2
         c = 1.0 + i2
-        r_ref[...] = c * (eye - (2.0 * alpha) * gram_ref[...] + (alpha * alpha) * square) - i2 * eye
-        x_ref[...] = (c * alpha) * (2.0 * eye - alpha * gram_ref[...])
+        r2 = c * (eye - (2.0 * alpha) * gram_ref[...] + (alpha * alpha) * square) - i2 * eye
+        x2 = (c * alpha) * (2.0 * eye - alpha * gram_ref[...])
+
+        def doubled_x(t, x, rp):
+            return (1.0 + 1.0 / t) * (x + dot3(pieces(x), rp))
+
+        def doubled_r(t, rp):
+            return (1.0 + 1.0 / t) * dot3(rp, rp) - (1.0 / t) * eye
+
+        t4 = 2.0 * t2 * t2 - 1.0
+        rp2 = pieces(r2)
+        x_ref[...] = doubled_x(t4, x2, rp2)
+        r_ref[...] = doubled_r(t4, rp2)
 
         def double(_, t):
             t = 2.0 * t * t - 1.0
-            it = 1.0 / t
-            x = x_ref[...]
             rp = pieces(r_ref[...])
-            x_ref[...] = (1.0 + it) * (x + dot3(pieces(x), rp))
-            r_ref[...] = (1.0 + it) * dot3(rp, rp) - it * eye
+            x_ref[...] = doubled_x(t, x_ref[...], rp)
+            r_ref[...] = doubled_r(t, rp)
             return t
 
-        t = lax.fori_loop(0, doublings, double, t2)
+        t = lax.fori_loop(0, doublings, double, t4)
         t = 2.0 * t * t - 1.0
-        x = x_ref[...]
-        x = (1.0 + 1.0 / t) * (x + dot3(pieces(x), pieces(r_ref[...])))
+        x = doubled_x(t, x_ref[...], pieces(r_ref[...]))
         x_ref[...] = x
         xp = pieces(x)
 

time: 51.1 us -> 51.1 us (level)
  no operation moved by 1% of the time
where the time goes in v9:
time: 51.1 us; the launch traced here: 50.9 us
  blocking collectives  30.1 us (59%)
  Pallas kernels  16.5 us (32%)
  starting transfers between devices  3.04 us (6%)
  between operations  0.68 us (1%)
  waiting for transfers between devices  0.52 us (1%)
    all_to_all x1, blocking collectives, body(): lax.all_to_all(sent, 'rows', 0, 0, tiled=True, axis_index_groups=members)  16 us
    all_to_all x1, blocking collectives, body(): lax.all_to_all(jnp.broadcast_to(own_lines[None], (2 * owners * parts, lin...  14.1 us
    pallas_call x1, Pallas kernels, project(): pl.pallas_call(functools.partial(project_kernel, chunk, owner, lines), ou...  8.87 us
    pallas_call x1, Pallas kernels, solve(): pl.pallas_call(functools.partial(solve_kernel, core_of), out_shape=(jax.S...  6.95 us
    ppermute x1, starting transfers between devices, body(): lax.ppermute(gathered, axes, [(i, i ^ 1) for i in range(times * rows)])  3.04 us
  transfers between devices with their start and end apart: 1, of which 1 were waited for; matrix products, arithmetic and copies ran while one was open for 0% of the time, Pallas kernels for 1%

profile of v9, /device:TPU:1, one launch (start us, length us, event | category | flops | bytes accessed | tf_op | source)
XLA Modules:
  0.0 50.9 jit_solution(2997452060348612284)
XLA Ops:
  0.6 0.0 copy-start.1
  0.6 0.0 copy-start
  0.7 8.9 %project.1 = f32[16,32,128]{2,1,0:T(8,128)S(1)} custom-call(bf16[32768,256]{1,0:T(8,128)(2,1)} %modes_hbm.1, bf16[32768,128]{1,0:T(8,128)(2,1)} %snaps_hbm.1), custom_call_target="tpu_custom_call" | custom-call | tf_op jit(solution)/shard_map/project/pallas_call | solution.py:310
  9.5 16.0 %all_to_all.10 = f32[16,32,128]{2,1,0:T(8,128)S(1)} all-to-all(f32[16,32,128]{2,1,0:T(8,128)S(1)} %project.1), channel_id=1, replica_groups={{0,8,32,40,4,12,36,44,16,24,48,56,20,28,52,60},{64,72,96,104,68,76,100,..., dimensions={0} | all-to-all | bytes 524288 | tf_op jit(solution)/shard_map/all_to_all | solution.py:361
  25.5 0.1 broadcast_in_dim.2
  25.6 14.1 %all_to_all.11 = f32[32,32,128]{2,1,0:T(8,128)S(1)} all-to-all(f32[32,32,128]{2,1,0:T(8,128)S(1)} %broadcast_in_dim.2), channel_id=1, replica_groups={{0,2,64,66,4,6,68,70,16,18,80,82,20,22,84,86,32,34,96,98,36,38,100,102,..., dimensions={0} | all-to-all | bytes 1048576 | tf_op jit(solution)/shard_map/all_to_all | solution.py:364
  39.7 3.0 %collective-permute-start = (f32[8,2,32,128]{3,2,1,0:T(8,128)S(1)}, f32[8,2,32,128]{3,2,1,0:T(8,128)S(1)}, u32[]{:S(2)}, u32[]{:S(2)}) collective-permute-start(f32[8,2,32,128]{3,2,1,0:T(8,128)S(1)} %reduce_sum.19.own_ref), channel_id=1, source_target_pairs={{0,1},{1,0},{2,3},{3,2},{4,5},{5,4},{6,7},{7,6},{8,9},{9,8},{10,11... | collective-permute-start | bytes 786440 | tf_op jit(solution)/shard_map/ppermute | solution.py:374
  42.8 0.6 %own_sums.1 = (f32[256,256]{1,0:T(8,128)S(1)}, f32[256,256]{1,0:T(8,128)S(1)}) custom-call(f32[8,2,32,128]{3,2,1,0:T(8,128)S(1)} %reduce_sum.19.own_ref), custom_call_target="tpu_custom_call" | custom-call | flops 402653184 | bytes 786432 | tf_op jit(solution)/shard_map/own_sums/pallas_call | solution.py:104
  43.4 0.5 %collective-permute-done.other_ref = f32[8,2,32,128]{3,2,1,0:T(8,128)S(1)} collective-permute-done((f32[8,2,32,128]{3,2,1,0:T(8,128)S(1)}, f32[8,2,32,128]{3,2,1,0:T(8,128)S(1)}, u32[]{:S(2)}, u32[]{:S(2)}) %collective-permute-start) | collective-permute-done | bytes 262176 | tf_op jit(solution)/shard_map/ppermute | solution.py:374
  43.9 0.0 copy-done.1
  43.9 0.0 copy-done
  43.9 6.9 %solve.1 = (f32[256,256]{1,0:T(8,128)}, f32[3,256]{1,0:T(4,128)}, f32[3]{0:T(128)}) custom-call(f32[8,2,32,128]{3,2,1,0:T(8,128)S(1)} %reduce_sum.19.own_ref, f32[8,2,32,128]{3,2,1,0:T(8,128)S(1)} %collective-permute-done.other_ref, f32[256,256]{1,0:T(8,128)S(1)} %get-tuple-element.5.gram_own_ref, f32[256,256]{1,0:T(8,128)S(1)} %get-tuple-element.6.cross_own_ref, ...), custom_call_target="tpu_custom_call" | custom-call | tf_op jit(solution)/shard_map/solve/pallas_call | solution.py:251
  (2 shorter events, 0.1 us)
Async XLA Ops:
  0.6 43.3 %copy-start.1 = (f32[3]{0:T(128)S(1)}, f32[3]{0:T(128)}, u32[]{:S(2)}) copy-start(f32[3]{0:T(128)} %val_ref.1) | copy-start | bytes 40
  0.6 43.3 %copy-start = (f32[3,256]{1,0:T(4,128)S(1)}, f32[3,256]{1,0:T(4,128)}, u32[]{:S(2)}) copy-start(f32[3,256]{1,0:T(4,128)} %vec_ref.1) | copy-start | bytes 9220
  39.7 4.2 %collective-permute-start = (f32[8,2,32,128]{3,2,1,0:T(8,128)S(1)}, f32[8,2,32,128]{3,2,1,0:T(8,128)S(1)}, u32[]{:S(2)}, u32[]{:S(2)}) collective-permute-start(f32[8,2,32,128]{3,2,1,0:T(8,128)S(1)} %reduce_sum.19.own_ref), channel_id=1, source_target_pairs={{0,1},{1,0},{2,3},{3,2},{4,5},{5,4},{6,7},{7,6},{8,9},{9,8},{10,11... | collective-permute-start | bytes 786440 | tf_op jit(solution)/shard_map/ppermute | solution.py:374
